TPU v7x, 8 devices: a whole 2x2x1 slice. The times are simulated.
8 devices in a mesh: dp: 1 (over z), y: 2 (over y), x: 4 (over x, core).
Axes of the slice: x: 2, y: 2, z: 1, core: 2. Of those that a mesh axis runs over, the one named last changes fastest.
Arguments:
- hidden: bfloat16 [256, 2560], P('dp', 'x')
- positions: int32 [256], P('dp')
- k_cache: bfloat16 [2, 256, 256, 8, 128], P(None, ('dp', 'x'), None, 'y')
- v_cache: bfloat16 [2, 256, 256, 8, 128], P(None, ('dp', 'x'), None, 'y')
- g_attn: bfloat16 [2, 2560], P(None, 'x')
- g_mlp: bfloat16 [2, 2560], P(None, 'x')
- q_gain: bfloat16 [2, 128], replicated
- k_gain: bfloat16 [2, 128], replicated
- w_q: bfloat16 [2, 2560, 4096], P(None, 'x', 'y')
- w_k: bfloat16 [2, 2560, 1024], P(None, 'x', 'y')
- w_v: bfloat16 [2, 2560, 1024], P(None, 'x', 'y')
- w_o: bfloat16 [2, 4096, 2560], P(None, 'y', 'x')
- w_gate: bfloat16 [2, 2560, 9728], P(None, 'x', 'y')
- w_up: bfloat16 [2, 2560, 9728], P(None, 'x', 'y')
- w_down: bfloat16 [2, 9728, 2560], P(None, 'y', 'x')
Outputs:
- output 1: bfloat16 [256, 2560], P('dp', 'x')
- output 2: bfloat16 [2, 256, 256, 8, 128], P(None, ('dp', 'x'), None, 'y')
- output 3: bfloat16 [2, 256, 256, 8, 128], P(None, ('dp', 'x'), None, 'y')
All inputs are finite; a program needn't handle non-finite values.
Results may differ from a plain program's by a relative error of at most 0.02.
Values are sent between devices in bfloat16 or wider.
A program may use at most 1 GiB of HBM per device.

v0:
```python
import jax
import jax.numpy as jnp
from jax import lax
from jax.sharding import PartitionSpec as P

HEAD_DIM = 128
NORM_EPS = 1e-6
ROPE_BASE = 1000000.0


def rope_tables(positions):
    half_dim = HEAD_DIM // 2
    inv_freq = jnp.power(ROPE_BASE, -2.0 * jnp.arange(half_dim, dtype=jnp.float32) / HEAD_DIM)
    angles = positions.astype(jnp.float32)[:, None] * inv_freq[None, :]
    return jnp.cos(angles), jnp.sin(angles)


def head_norm_rope(head_vals, norm_gain, cos_tab, sin_tab):
    heads_f32 = head_vals.astype(jnp.float32)
    mean_sq = jnp.mean(heads_f32 * heads_f32, axis=-1, keepdims=True)
    normed = heads_f32 * lax.rsqrt(mean_sq + NORM_EPS) * norm_gain.astype(jnp.float32)
    half_dim = HEAD_DIM // 2
    first_half = normed[..., :half_dim]
    second_half = normed[..., half_dim:]
    cos_b = cos_tab[:, None, :]
    sin_b = sin_tab[:, None, :]
    return jnp.concatenate([first_half * cos_b - second_half * sin_b, second_half * cos_b + first_half * sin_b], axis=-1).astype(jnp.bfloat16)


def sharded_rms(hidden, norm_gain, model_dim):
    hidden_f32 = hidden.astype(jnp.float32)
    sum_sq = lax.psum(jnp.sum(hidden_f32 * hidden_f32, axis=1, keepdims=True), 'x')
    return (hidden_f32 * lax.rsqrt(sum_sq / model_dim + NORM_EPS) * norm_gain.astype(jnp.float32)).astype(jnp.bfloat16)


def cache_attention(q_rot, k_cache, v_cache, k_rot, v_proj, my_pos):
    batch_rows, q_local, head_dim = q_rot.shape
    cache_len = k_cache.shape[1]
    kv_local = k_cache.shape[2]
    slot_ids = lax.broadcasted_iota(jnp.int32, (1, cache_len), 1)
    slot_hit = (slot_ids == my_pos[:, None])[:, :, None, None]
    k_new = jnp.where(slot_hit, k_rot[:, None], k_cache)
    v_new = jnp.where(slot_hit, v_proj[:, None], v_cache)
    q_grouped = q_rot.reshape(batch_rows, kv_local, q_local // kv_local, head_dim)
    scores = jnp.einsum('bkge,blke->bkgl', q_grouped, k_new, preferred_element_type=jnp.float32) * (HEAD_DIM ** -0.5)
    valid_slot = (slot_ids <= my_pos[:, None])[:, None, None, :]
    scores = jnp.where(valid_slot, scores, -1e30)
    att_probs = jax.nn.softmax(scores, axis=-1).astype(jnp.bfloat16)
    attn_heads = jnp.einsum('bkgl,blke->bkge', att_probs, v_new, preferred_element_type=jnp.float32).astype(jnp.bfloat16)
    return attn_heads.reshape(batch_rows, q_local * head_dim), k_new, v_new


def solution(mesh):
    group_size = mesh.shape['x']
    cache_spec = P(None, ('dp', 'x'), None, 'y', None)
    col_spec = P(None, 'x', 'y')
    row_spec = P(None, 'y', 'x')
    in_specs = (P('dp', 'x'), P('dp'), cache_spec, cache_spec, P(None, 'x'), P(None, 'x'), P(), P(), col_spec, col_spec, col_spec, row_spec, col_spec, col_spec, row_spec)
    out_specs = (P('dp', 'x'), cache_spec, cache_spec)

    def device_step(hidden, positions, k_cache, v_cache, g_attn, g_mlp, q_gain, k_gain, w_q, w_k, w_v, w_o, w_gate, w_up, w_down):
        model_dim = hidden.shape[1] * group_size
        local_batch = k_cache.shape[1]
        kv_local = k_cache.shape[3]
        q_cols = w_q.shape[2]
        kv_cols = w_k.shape[2]
        ffn_local = w_gate.shape[2]
        my_pos = lax.dynamic_slice_in_dim(positions, lax.axis_index('x') * local_batch, local_batch)
        cos_tab, sin_tab = rope_tables(my_pos)
        k_list = []
        v_list = []
        for layer_idx in range(k_cache.shape[0]):
            normed = sharded_rms(hidden, g_attn[layer_idx], model_dim)
            proj_parts = jnp.concatenate([
                jnp.dot(normed, w_q[layer_idx], preferred_element_type=jnp.float32).astype(jnp.bfloat16),
                jnp.dot(normed, w_k[layer_idx], preferred_element_type=jnp.float32).astype(jnp.bfloat16),
                jnp.dot(normed, w_v[layer_idx], preferred_element_type=jnp.float32).astype(jnp.bfloat16)], axis=1)
            proj_sum = lax.psum_scatter(proj_parts, 'x', scatter_dimension=0, tiled=True)
            q_proj = proj_sum[:, :q_cols].reshape(local_batch, q_cols // HEAD_DIM, HEAD_DIM)
            k_proj = proj_sum[:, q_cols:q_cols + kv_cols].reshape(local_batch, kv_local, HEAD_DIM)
            v_proj = proj_sum[:, q_cols + kv_cols:].reshape(local_batch, kv_local, HEAD_DIM)
            q_rot = head_norm_rope(q_proj, q_gain[layer_idx], cos_tab, sin_tab)
            k_rot = head_norm_rope(k_proj, k_gain[layer_idx], cos_tab, sin_tab)
            attn_local, k_new, v_new = cache_attention(q_rot, k_cache[layer_idx], v_cache[layer_idx], k_rot, v_proj, my_pos)
            attn_all = lax.all_gather(attn_local, 'x', axis=0, tiled=True)
            attn_out = lax.psum(jnp.dot(attn_all, w_o[layer_idx], preferred_element_type=jnp.float32).astype(jnp.bfloat16), 'y')
            mid_hidden = (hidden.astype(jnp.float32) + attn_out.astype(jnp.float32)).astype(jnp.bfloat16)
            normed_mlp = sharded_rms(mid_hidden, g_mlp[layer_idx], model_dim)
            gate_up = lax.psum(jnp.concatenate([
                jnp.dot(normed_mlp, w_gate[layer_idx], preferred_element_type=jnp.float32).astype(jnp.bfloat16),
                jnp.dot(normed_mlp, w_up[layer_idx], preferred_element_type=jnp.float32).astype(jnp.bfloat16)], axis=1), 'x')
            act_val = (jax.nn.silu(gate_up[:, :ffn_local].astype(jnp.float32)) * gate_up[:, ffn_local:].astype(jnp.float32)).astype(jnp.bfloat16)
            mlp_out = lax.psum(jnp.dot(act_val, w_down[layer_idx], preferred_element_type=jnp.float32).astype(jnp.bfloat16), 'y')
            hidden = (mid_hidden.astype(jnp.float32) + mlp_out.astype(jnp.float32)).astype(jnp.bfloat16)
            k_list.append(k_new)
            v_list.append(v_new)
        return hidden, jnp.stack(k_list), jnp.stack(v_list)

    return jax.shard_map(device_step, mesh=mesh, in_specs=in_specs, out_specs=out_specs, check_vma=False)
```

profile of v0, /device:TPU:0, one launch (start us, length us, event | category | flops | bytes accessed | tf_op | source)
XLA Modules:
  0.0 576.8 jit_solution(6029611136042463903)
XLA Ops:
  7.2 1.1 fusion.98
  8.3 8.7 %psum.70 = f32[256,1]{0,1:T(1,128)S(1)} all-reduce(f32[256,1]{0,1:T(1,128)S(1)} %bitcast.107), channel_id=1, replica_groups=mesh['dp'=1,'y'=2,'x'=4] {'x'}, use_global_device_ids=true, to_apply=%region_1.0 | all-reduce | flops 256 | bytes 2048 | tf_op jit(solution)/shard_map/psum | solution.py:32
  17.1 0.8 convert_reduce_fusion.3
  17.9 1.6 convolution_convert_fusion.7
  19.5 1.6 convolution_convert_fusion.6
  21.2 2.9 fusion.46
  24.1 1.3 pad_maximum_fusion.4
  25.7 0.2 multiply_cosine_fusion
  25.9 22.0 %reduce-scatter.3.cloned.1.call-done = bf16[64,3072]{1,0:T(8,128)(2,1)} async-done(((bf16[256,3072]{1,0:T(8,128)(2,1)}), bf16[64,3072]{1,0:T(8,128)(2,1)}) %reduce-scatter.3.cloned.1.call-update) | async-done | bytes 393232 | tf_op jit(solution)/shard_map/reduce_scatter | solution.py:78
  47.9 0.9 slice_convert_fusion.1
  48.9 0.1 multiply_reduce_fusion.3
  49.1 1.0 convert_bitcast_fusion.1
  50.2 0.2 multiply_reduce_fusion.1
  50.5 0.2 multiply_multiply_fusion.1
  50.7 0.2 subtract_convert_fusion.3
  50.9 0.2 subtract_convert_fusion.1
  51.3 25.9 %bitcast_select_fusion.3 = (bf16[64,256,4,128]{3,2,1,0:T(4,128)(2,1)}, bf16[64,256,4,128]{3,2,1,0:T(4,128)(2,1)}) fusion(pred[64,256]{1,0:T(8,128)(4,1)S(1)} %get-tuple-element.42, bf16[2,64,256,4,128]{4,3,2,1,0:T(4,128)(2,1)} %param.17, bf16[64,4,128]{2,1,0:T(4,128)(2,1)S(1)} %pad_maximum_fusion.6, bf16[2,64,256,4,128]{4,3,2,1,0:T(4,128)(2,1)} %param.18, ...), kind=kLoop, calls=%fused_computation.7 | loop fusion | flops 16777216 | bytes 67256320 | tf_op jit(solution)/shard_map/jit(_where)/select_n | solution.py:42
  77.2 10.5 %fusion.144 = (f32[64,4,4]{2,1,0:T(4,128)S(1)}, f32[64,4,4,256]{3,2,1,0:T(4,128)S(1)}) fusion(bf16[64,256,4,128]{3,2,1,0:T(4,128)(2,1)} %get-tuple-element.33, pred[64,256]{1,0:T(8,128)(4,1)S(1)} %get-tuple-element.41, bf16[64,4,4,64]{3,2,1,0:T(4,128)(2,1)S(1)} %bitcast.104, bf16[64,4,4,64]{3,2,1,0:T(4,128)(2,1)S(1)} %bitcast.103), kind=kOutput, calls=%fused_computation.188 | convolution fusion | flops 68681984 | bytes 18108416 | tf_op jit(solution)/shard_map/sub | solution.py:48
  87.7 8.2 %fusion.86 = bf16[64,4,4,128]{3,2,1,0:T(4,128)(2,1)S(1)} fusion(bf16[64,256,4,128]{3,2,1,0:T(4,128)(2,1)} %get-tuple-element.34, f32[64,4,4,256]{3,2,1,0:T(4,128)S(1)} %get-tuple-element.44, f32[64,4,4]{2,1,0:T(4,128)S(1)} %get-tuple-element.43), kind=kOutput, calls=%fused_computation.86 | convolution fusion | flops 67764224 | bytes 18092032 | tf_op jit(solution)/shard_map/bkgl,blke->bkge/dot_general | solution.py:49
  95.9 0.9 reshape.216
  96.9 13.8 %all-gather.3.cloned.1.call-done = bf16[256,2048]{1,0:T(8,128)(2,1)} async-done(((bf16[64,2048]{1,0:T(8,128)(2,1)}), bf16[256,2048]{1,0:T(8,128)(2,1)}) %all-gather.3.cloned.1.call-update) | async-done | bytes 1048592 | tf_op jit(solution)/shard_map/all_gather | solution.py:85
  110.7 3.8 fusion.70
  114.6 18.7 %all-reduce.7.cloned.1.call-done = bf16[256,640]{1,0:T(8,128)(2,1)} async-done(((bf16[256,640]{1,0:T(8,128)(2,1)}), bf16[256,640]{1,0:T(8,128)(2,1)}) %all-reduce.7.cloned.1.call-update) | async-done | bytes 327696 | tf_op jit(solution)/shard_map/psum | solution.py:86
  133.3 1.2 fusion.102
  134.5 7.0 %psum.72 = f32[256,1]{0,1:T(1,128)S(1)} all-reduce(f32[256,1]{0,1:T(1,128)S(1)} %bitcast.105), channel_id=1, replica_groups=mesh['dp'=1,'y'=2,'x'=4] {'x'}, use_global_device_ids=true, to_apply=%region_9.10 | all-reduce | flops 256 | bytes 2048 | tf_op jit(solution)/shard_map/psum | solution.py:32
  141.5 4.9 convolution_convert_fusion.2
  146.4 4.9 convolution_convert_fusion.3
  151.4 2.6 pad_maximum_fusion.2
  154.1 91.7 %all-reduce.9.cloned.1.call-done = bf16[256,9728]{1,0:T(8,128)(2,1)} async-done(((bf16[256,9728]{1,0:T(8,128)(2,1)}), bf16[256,9728]{1,0:T(8,128)(2,1)}) %all-reduce.9.cloned.1.call-update) | async-done | bytes 4980752 | tf_op jit(solution)/shard_map/psum | solution.py:89
  245.8 7.4 %fusion.76 = bf16[256,640]{1,0:T(8,128)(2,1)} fusion(bf16[2,4864,640]{2,1,0:T(8,128)(2,1)} %param.29, bf16[256,9728]{1,0:T(8,128)(2,1)} %all-reduce.9.cloned.1.call-done), kind=kOutput, calls=%fused_computation.84 | convolution fusion | flops 1603960832 | bytes 11534336 | tf_op jit(solution)/shard_map/dot_general | solution.py:93
  253.2 18.9 %all-reduce.11.cloned.1.call-done = bf16[256,640]{1,0:T(8,128)(2,1)} async-done(((bf16[256,640]{1,0:T(8,128)(2,1)}), bf16[256,640]{1,0:T(8,128)(2,1)}) %all-reduce.11.cloned.1.call-update) | async-done | bytes 327696 | tf_op jit(solution)/shard_map/psum | solution.py:93
  272.1 1.2 fusion.106
  273.3 6.9 %psum.75 = f32[256,1]{0,1:T(1,128)S(1)} all-reduce(f32[256,1]{0,1:T(1,128)S(1)} %bitcast.108), channel_id=1, replica_groups=mesh['dp'=1,'y'=2,'x'=4] {'x'}, use_global_device_ids=true, to_apply=%region_13.14 | all-reduce | flops 256 | bytes 2048 | tf_op jit(solution)/shard_map/psum | solution.py:32
  280.2 1.1 fusion.108
  281.3 0.4 convolution_convert_fusion.4
  281.7 1.5 convolution_convert_fusion.5
  283.1 2.7 fusion.49
  285.9 1.3 pad_maximum_fusion.5
  287.2 0.3 all-gather.5.cloned.1.call-start
  287.4 21.3 %reduce-scatter.5.cloned.1.call-done = bf16[64,3072]{1,0:T(8,128)(2,1)} async-done(((bf16[256,3072]{1,0:T(8,128)(2,1)}), bf16[64,3072]{1,0:T(8,128)(2,1)}) %reduce-scatter.5.cloned.1.call-update) | async-done | bytes 393232 | tf_op jit(solution)/shard_map/reduce_scatter | solution.py:78
  308.8 0.9 slice_convert_fusion
  309.7 0.1 multiply_reduce_fusion.2
  310.0 0.2 subtract_convert_fusion.2
  310.2 1.0 convert_bitcast_fusion
  311.3 0.2 multiply_reduce_fusion
  311.5 0.2 multiply_multiply_fusion
  311.7 0.2 subtract_convert_fusion
  312.1 26.0 %bitcast_select_fusion.1 = (bf16[64,256,4,128]{3,2,1,0:T(4,128)(2,1)}, bf16[64,256,4,128]{3,2,1,0:T(4,128)(2,1)}) fusion(pred[64,256]{1,0:T(8,128)(4,1)S(1)} %get-tuple-element.42, bf16[2,64,256,4,128]{4,3,2,1,0:T(4,128)(2,1)} %param.17, bf16[64,4,128]{2,1,0:T(4,128)(2,1)S(1)} %pad_maximum_fusion.7, bf16[2,64,256,4,128]{4,3,2,1,0:T(4,128)(2,1)} %param.18, ...), kind=kLoop, calls=%fused_computation.5 | loop fusion | flops 16777216 | bytes 67256320 | tf_op jit(solution)/shard_map/jit(_where)/select_n | solution.py:42
  338.1 10.5 %fusion.145 = (f32[64,4,4]{2,1,0:T(4,128)S(1)}, f32[64,4,4,256]{3,2,1,0:T(4,128)S(1)}) fusion(bf16[64,256,4,128]{3,2,1,0:T(4,128)(2,1)} %get-tuple-element.31, pred[64,256]{1,0:T(8,128)(4,1)S(1)} %get-tuple-element.41, bf16[64,4,4,64]{3,2,1,0:T(4,128)(2,1)S(1)} %bitcast.102, bf16[64,4,4,64]{3,2,1,0:T(4,128)(2,1)S(1)} %bitcast.101), kind=kOutput, calls=%fused_computation.189 | convolution fusion | flops 68681984 | bytes 18108416 | tf_op jit(solution)/shard_map/sub | solution.py:48
  348.6 8.2 %fusion.89 = bf16[64,4,4,128]{3,2,1,0:T(4,128)(2,1)S(1)} fusion(bf16[64,256,4,128]{3,2,1,0:T(4,128)(2,1)} %get-tuple-element.32, f32[64,4,4,256]{3,2,1,0:T(4,128)S(1)} %get-tuple-element.46, f32[64,4,4]{2,1,0:T(4,128)S(1)} %get-tuple-element.45), kind=kOutput, calls=%fused_computation.87 | convolution fusion | flops 67764224 | bytes 18092032 | tf_op jit(solution)/shard_map/bkgl,blke->bkge/dot_general | solution.py:49
  356.7 0.9 reshape.217
  357.7 13.8 %all-gather.5.cloned.1.call-done = bf16[256,2048]{1,0:T(8,128)(2,1)} async-done(((bf16[64,2048]{1,0:T(8,128)(2,1)}), bf16[256,2048]{1,0:T(8,128)(2,1)}) %all-gather.5.cloned.1.call-update) | async-done | bytes 1048592 | tf_op jit(solution)/shard_map/all_gather | solution.py:85
  371.5 3.8 fusion.73
  375.4 18.7 %all-reduce.13.cloned.1.call-done = bf16[256,640]{1,0:T(8,128)(2,1)} async-done(((bf16[256,640]{1,0:T(8,128)(2,1)}), bf16[256,640]{1,0:T(8,128)(2,1)}) %all-reduce.13.cloned.1.call-update) | async-done | bytes 327696 | tf_op jit(solution)/shard_map/psum | solution.py:86
  394.1 1.2 fusion.110
  395.3 7.1 %psum.77 = f32[256,1]{0,1:T(1,128)S(1)} all-reduce(f32[256,1]{0,1:T(1,128)S(1)} %bitcast.109), channel_id=1, replica_groups=mesh['dp'=1,'y'=2,'x'=4] {'x'}, use_global_device_ids=true, to_apply=%region_21.22 | all-reduce | flops 256 | bytes 2048 | tf_op jit(solution)/shard_map/psum | solution.py:32
  402.5 4.9 convolution_convert_fusion
  407.4 4.9 convolution_convert_fusion.1
  412.3 2.6 pad_maximum_fusion.3
  415.0 43.9 %broadcast_select_fusion.1 = (bf16[1,64,256,4,128]{4,3,2,1,0:T(4,128)(2,1)}, bf16[1,64,256,4,128]{4,3,2,1,0:T(4,128)(2,1)}, bf16[1,64,256,4,128]{4,3,2,1,0:T(4,128)(2,1)}, bf16[1,64,256,4,128]{4,3,2,1,0:T(4,128)(2,1)}) fusion(pred[64,256]{1,0:T(8,128)(4,1)S(1)} %get-tuple-element.42, bf16[2,64,256,4,128]{4,3,2,1,0:T(4,128)(2,1)} %param.18, ...), kind=kLoop, calls=%fused_computation.17 | loop fusion | flops 33554432 | bytes 134496256 | tf_op jit(solution)/shard_map/jit(_where)/select_n | solution.py:43
  458.9 47.9 %all-reduce.15.cloned.1.call-done = bf16[256,9728]{1,0:T(8,128)(2,1)} async-done(((bf16[256,9728]{1,0:T(8,128)(2,1)}), bf16[256,9728]{1,0:T(8,128)(2,1)}) %all-reduce.15.cloned.1.call-update) | async-done | bytes 4980752 | tf_op jit(solution)/shard_map/psum | solution.py:89
  506.7 7.4 %fusion.81 = bf16[256,640]{1,0:T(8,128)(2,1)} fusion(bf16[2,4864,640]{2,1,0:T(8,128)(2,1)} %param.29, bf16[256,9728]{1,0:T(8,128)(2,1)} %all-reduce.15.cloned.1.call-done), kind=kOutput, calls=%fused_computation.85 | convolution fusion | flops 1603960832 | bytes 11534336 | tf_op jit(solution)/shard_map/dot_general | solution.py:93
  514.1 53.6 %pad_maximum_fusion = (bf16[2,64,256,4,128]{4,3,2,1,0:T(4,128)(2,1)}, bf16[2,64,256,4,128]{4,3,2,1,0:T(4,128)(2,1)}) fusion(bf16[1,64,256,4,128]{4,3,2,1,0:T(4,128)(2,1)} %get-tuple-element.29, bf16[1,64,256,4,128]{4,3,2,1,0:T(4,128)(2,1)} %get-tuple-element.30, bf16[1,64,256,4,128]{4,3,2,1,0:T(4,128)(2,1)} %get-tuple-element.14, ...), kind=kLoop, calls=%fused_computation.2 | loop fusion | flops 33554432 | bytes 134217728 | tf_op jit(solution)/shard_map/stack | solution.py:97
  567.7 1.8 fusion.113
  (58 shorter events, 1.7 us)
Async XLA Ops:
  7.2 40.8 %reduce-scatter.3.cloned.1.call-start = ((), (), s32[]{:S(2)}) async-start(), calls=%async_computation.2 | async-start | bytes 1966080 | tf_op jit(solution)/shard_map/reduce_scatter | solution.py:78
  19.5 6.0 %copy-start.5 = (s32[256]{0:T(256)S(1)}, s32[256]{0:T(256)}, u32[]{:S(2)}) copy-start(s32[256]{0:T(256)} %param.16) | copy-start | bytes 3076
  19.5 6.1 %copy-start.3 = (bf16[2,128]{1,0:T(2,128)(2,1)S(1)}, bf16[2,128]{1,0:T(2,128)(2,1)}, u32[]{:S(2)}) copy-start(bf16[2,128]{1,0:T(2,128)(2,1)} %param.21) | copy-start | bytes 1540
  19.5 6.1 %copy-start.4 = (bf16[2,128]{1,0:T(2,128)(2,1)S(1)}, bf16[2,128]{1,0:T(2,128)(2,1)}, u32[]{:S(2)}) copy-start(bf16[2,128]{1,0:T(2,128)(2,1)} %param.22) | copy-start | bytes 1540
  25.4 85.3 %all-gather.3.cloned.1.call-start = ((), (), s32[]{:S(2)}) async-start(), calls=%async_computation.3 | async-start | bytes 1310720 | tf_op jit(solution)/shard_map/all_gather | solution.py:85
  95.9 18.7 %copy-start.2 = (bf16[2,640]{1,0:T(2,128)(2,1)S(1)}, bf16[2,640]{1,0:T(2,128)(2,1)}, u32[]{:S(2)}) copy-start(bf16[2,640]{1,0:T(2,128)(2,1)} %param.20) | copy-start | bytes 7684
  95.9 37.4 %copy-start.1 = (bf16[256,640]{1,0:T(8,128)(2,1)S(1)}, bf16[256,640]{1,0:T(8,128)(2,1)}, u32[]{:S(2)}) copy-start(bf16[256,640]{1,0:T(8,128)(2,1)} %param.15) | copy-start | bytes 983044
  96.8 36.5 %all-reduce.7.cloned.1.call-start = ((), (), s32[]{:S(2)}) async-start(), calls=%async_computation.4 | async-start | bytes 655360 | tf_op jit(solution)/shard_map/psum | solution.py:86
  114.5 131.3 %all-reduce.9.cloned.1.call-start = ((), (), s32[]{:S(2)}) async-start(), calls=%async_computation.5 | async-start | bytes 9961472 | tf_op jit(solution)/shard_map/psum | solution.py:89
  154.0 127.3 %copy-start.6 = (bf16[2,640,512]{2,1,0:T(8,128)(2,1)S(1)}, bf16[2,640,512]{2,1,0:T(8,128)(2,1)}, u32[]{:S(2)}) copy-start(bf16[2,640,512]{2,1,0:T(8,128)(2,1)} %param.25) | copy-start | bytes 3932164
  154.0 118.1 %all-reduce.11.cloned.1.call-start = ((), (), s32[]{:S(2)}) async-start(), calls=%async_computation.6 | async-start | bytes 655360 | tf_op jit(solution)/shard_map/psum | solution.py:93
  253.2 55.6 %reduce-scatter.5.cloned.1.call-start = ((), (), s32[]{:S(2)}) async-start(), calls=%async_computation.7 | async-start | bytes 1966080 | tf_op jit(solution)/shard_map/reduce_scatter | solution.py:78
  287.2 84.4 %all-gather.5.cloned.1.call-start = ((), (), s32[]{:S(2)}) async-start(), calls=%async_computation.8 | async-start | bytes 1310720 | tf_op jit(solution)/shard_map/all_gather | solution.py:85
  356.7 37.4 %copy-start = (bf16[256,640]{1,0:T(8,128)(2,1)S(1)}, bf16[256,640]{1,0:T(8,128)(2,1)}, u32[]{:S(2)}) copy-start(bf16[256,640]{1,0:T(8,128)(2,1)} %all-reduce.11.cloned.1.call-done) | copy-start | bytes 983044
  357.6 36.5 %all-reduce.13.cloned.1.call-start = ((), (), s32[]{:S(2)}) async-start(), calls=%async_computation.9 | async-start | bytes 655360 | tf_op jit(solution)/shard_map/psum | solution.py:86
  375.3 131.4 %all-reduce.15.cloned.1.call-start = ((), (), s32[]{:S(2)}) async-start(), calls=%async_computation.10 | async-start | bytes 9961472 | tf_op jit(solution)/shard_map/psum | solution.py:89
  415.0 152.7 %all-reduce.17.cloned.1.call-start = ((), (), s32[]{:S(2)}) async-start(), calls=%async_computation.11 | async-start | bytes 655360 | tf_op jit(solution)/shard_map/psum | solution.py:93
Sparse Core Ops, SparseCore 0:
  25.5 22.3 reduce-scatter.2
  96.9 13.7 all-gather.2
  114.6 18.6 all-reduce.6
  154.1 91.6 all-reduce.8
  253.3 18.8 all-reduce.10
  287.3 21.4 reduce-scatter.4
  357.8 13.7 all-gather.4
  375.5 18.6 all-reduce.12
  415.1 91.6 all-reduce.14
  514.2 18.8 all-reduce.16
where the time goes:
time: 586 us; the launch traced here: 577 us
  waiting for transfers between devices  267 us (46%)
  other arithmetic  172 us (29%)
  matrix products  90 us (15%)
  blocking collectives  29.8 us (5%)
  between operations  15 us (3%)
    psum x2, waiting for transfers between devices, device_step(): lax.psum(jnp.concatenate([jnp.dot(normed_mlp, w_gate[layer_idx], preferre...  140 us
    another operation x1, other arithmetic, device_step(): return (hidden, jnp.stack(k_list), jnp.stack(v_list))  53.6 us
    select_n x2, other arithmetic, cache_attention(): k_new = jnp.where(slot_hit, k_rot[:, None], k_cache)  51.9 us
    select_n x1, other arithmetic, cache_attention(): v_new = jnp.where(slot_hit, v_proj[:, None], v_cache)  43.9 us
    reduce_scatter x2, waiting for transfers between devices, device_step(): lax.psum_scatter(proj_parts, 'x', scatter_dimension=0, tiled=True)  43.4 us
    psum x2, waiting for transfers between devices, device_step(): lax.psum(jnp.dot(attn_all, w_o[layer_idx], preferred_element_type=jnp.flo...  37.4 us
    psum x4, blocking collectives, sharded_rms(): lax.psum(jnp.sum(hidden_f32 * hidden_f32, axis=1, keepdims=True), 'x')  29.8 us
    all_gather x2, waiting for transfers between devices, device_step(): attn_all = lax.all_gather(attn_local, 'x', axis=0, tiled=True)  27.7 us
  transfers between devices with their start and end apart: 10, of which 9 were waited for; matrix products, arithmetic and copies ran while one was open for 17% of the time, Pallas kernels for 0%

commit v1 on v0

v1 whole, which is shorter than its diff:
```python
import functools

import jax
import jax.numpy as jnp
from jax import lax
from jax.experimental import pallas as pl
from jax.experimental.pallas import tpu as pltpu
from jax.sharding import PartitionSpec as P

HEAD_DIM = 128
NORM_EPS = 1e-6
ROPE_BASE = 1000000.0
MESH = pl.DeviceIdType.MESH
BF16 = jnp.bfloat16
F32 = jnp.float32

NM = 1
CW = 256
IW = 2 * CW
O2, O3, O4, O5 = 1, 3, 5, 6
SB = 8
MASK = (0, 2, 1, 3)
POS = (0, 2, 1, 3)


def dot(a, b):
    return jnp.dot(a, b, preferred_element_type=F32)


def chain_kernel(head, tail, layer, model_dim, *refs):
    it = iter(refs)
    hid_in = next(it)
    if head:
        attn_in, g_mlp = next(it), next(it)
        wo_in, wg_in, wu_in, wd_in = (next(it).at[layer] for _ in range(4))
    if tail:
        tail_layer = layer + 1 if head else layer
        g_attn = next(it)
        wq_in, wk_in, wv_in = (next(it).at[tail_layer] for _ in range(3))
    if head:
        hid_out = next(it)
    if tail:
        qkv_out = next(it)
    h_buf, n_buf, stat_buf, keep_buf, own_buf, dsend, drecv, xsend, xrecv = (next(it) for _ in range(9))
    h_sem, st_ss, st_rs, d_ss, d_rs, x_ss, x_rs = (next(it) for _ in range(7))
    if head:
        attn_all, wo_buf, wgu_buf, wd_buf, acc_buf, act_all, y_send, y_recv = (next(it) for _ in range(8))
        ag_ss, ag_rs, y_ss, y_rs, act_ss, act_rs, wo_sem, wgu_sem, wd_sem, o_sem = (next(it) for _ in range(10))
    if tail:
        wqkv_buf, wqkv_sem = (next(it) for _ in range(2))

    me = lax.axis_index('x')
    yy = lax.axis_index('y')
    chip, core = lax.div(me, 2), lax.rem(me, 2)
    d1 = chip * 2 + (1 - core)
    d2 = (1 - chip) * 2 + core
    d3 = (1 - chip) * 2 + (1 - core)
    quarter = (me, d2, d1, d3)
    R = h_buf.shape[1] // 4
    M = 4 * R
    n_ffn = act_all.shape[0] // NM if head else 0
    n_mlp = n_ffn * NM
    n_qkv = 6

    barrier = pltpu.get_barrier_semaphore()
    for peer in ({'x': d1}, {'x': d2}, {'x': d3}, {'y': 1 - yy}):
        pl.semaphore_signal(barrier, inc=1, device_id=peer, device_id_type=MESH)

    def remote(src, dst, ss, rs, peer):
        return pltpu.make_async_remote_copy(src_ref=src, dst_ref=dst, send_sem=ss, recv_sem=rs, device_id=peer, device_id_type=MESH)

    def hid_copy(m, k):
        row = pl.multiple_of(quarter[k] * (NM * R) + m * R, R)
        return pltpu.make_async_copy(hid_in.at[pl.ds(row, R)], h_buf.at[m, pl.ds(k * R, R)], h_sem.at[m, k])

    for m in range(NM):
        for k in range(4):
            hid_copy(m, k).start()

    def wgu_copy(j):
        off = pl.multiple_of(j * CW, CW)
        return (pltpu.make_async_copy(wg_in.at[:, pl.ds(off, CW)], wgu_buf.at[j, :, pl.ds(0, CW)], wgu_sem.at[0, j]),
                pltpu.make_async_copy(wu_in.at[:, pl.ds(off, CW)], wgu_buf.at[j, :, pl.ds(CW, CW)], wgu_sem.at[1, j]))

    if head:
        wo_copy = pltpu.make_async_copy(wo_in, wo_buf, wo_sem)
        wd_copy = pltpu.make_async_copy(wd_in, wd_buf, wd_sem)
    if tail:
        wqkv_copies = [pltpu.make_async_copy(wq_in.at[:, pl.ds(j * IW, IW)], wqkv_buf.at[j], wqkv_sem.at[j]) for j in range(4)]
        wqkv_copies += [pltpu.make_async_copy(w, wqkv_buf.at[j], wqkv_sem.at[j]) for j, w in ((4, wk_in), (5, wv_in))]
    if head:
        wo_copy.start()

        def start_wgu(j, c):
            for cp in wgu_copy(j):
                cp.start()
            return c
        lax.fori_loop(0, n_ffn, start_wgu, 0)
        wd_copy.start()
    if tail:
        for cp in wqkv_copies:
            cp.start()

    def diag():
        return lax.broadcasted_iota(jnp.int32, (R, 128), 0) == lax.broadcasted_iota(jnp.int32, (R, 128), 1)

    def stat_send(kind, m, a):
        peer = (None, d1, d2, d3)[a]
        return remote(stat_buf.at[kind, m, 0], stat_buf.at[kind, m, a], st_ss.at[kind, m, a - 1], st_rs.at[kind, m, a - 1], {'x': peer})

    def stats_start(kind, m):
        for k in range(4):
            hv = h_buf[m, pl.ds(k * R, R), :].astype(F32)
            row_sum = jnp.sum(hv * hv, axis=1, keepdims=True)
            stat_buf[kind, m, 0, pl.ds(k, 1), :] = jnp.sum(jnp.where(diag(), row_sum, 0.0), axis=0, keepdims=True)
        for a in (1, 2, 3):
            stat_send(kind, m, a).start()

    def norm(kind, m, gain):
        for a in (1, 2, 3):
            stat_send(kind, m, a).wait()
        gain_row = gain.astype(F32)
        for k in range(4):
            total = stat_buf[kind, m, 0, pl.ds(k, 1), :]
            for a in (1, 2, 3):
                total = total + stat_buf[kind, m, a, pl.ds(POS[MASK[k] ^ a], 1), :]
            col = jnp.sum(jnp.where(diag(), total, 0.0), axis=1, keepdims=True)
            hv = h_buf[m, pl.ds(k * R, R), :].astype(F32)
            n_buf[m, pl.ds(k * R, R), :] = (hv * lax.rsqrt(col / model_dim + NORM_EPS) * gain_row).astype(BF16)

    def d_copy(s):
        return remote(dsend.at[s], drecv.at[s], d_ss.at[s], d_rs.at[s], {'x': d1})

    def x_copy(s):
        return remote(xsend.at[s], xrecv.at[s], x_ss.at[s], x_rs.at[s], {'x': d2})

    def stage1(s, m, w):
        part = dot(n_buf[m], w)
        keep_buf[lax.rem(s, keep_buf.shape[0])] = part[:2 * R]
        dsend[s] = part[2 * R:].astype(BF16)
        d_copy(s).start()

    def stage2(s):
        d_copy(s).wait_recv()
        slot = lax.rem(s, keep_buf.shape[0])
        xsend[s] = (keep_buf[slot, pl.ds(R, R), :] + drecv[s, pl.ds(R, R), :].astype(F32)).astype(BF16)
        x_copy(s).start()
        own_buf[lax.rem(s, own_buf.shape[0])] = keep_buf[slot, pl.ds(0, R), :] + drecv[s, pl.ds(0, R), :].astype(F32)

    def stage3(s):
        x_copy(s).wait_recv()
        return (own_buf[lax.rem(s, own_buf.shape[0])] + xrecv[s].astype(F32)).astype(BF16)

    def gather_copies(buf, i, ss, rs):
        own, other = buf.at[i, pl.ds(0, R)], buf.at[i, pl.ds(R, R)]
        return (lambda: remote(own, buf.at[i, pl.ds(2 * R, R)], ss.at[0, i], rs.at[0, i], {'x': d1}),
                lambda: remote(own, buf.at[i, pl.ds(R, R)], ss.at[1, i], rs.at[1, i], {'x': d2}),
                lambda: remote(other, buf.at[i, pl.ds(3 * R, R)], ss.at[2, i], rs.at[2, i], {'x': d1}))

    def attn_copies(m):
        return gather_copies(attn_all, m, ag_ss, ag_rs)

    def y_copy(kind, m):
        return remote(y_send.at[kind, m], y_recv.at[kind, m], y_ss.at[kind, m], y_rs.at[kind, m], {'y': 1 - yy})

    def y_start(kind, m, value):
        y_send[kind, m] = value.astype(BF16)
        y_copy(kind, m).start()

    def y_finish(kind, m):
        y_copy(kind, m).wait()
        total = (y_send[kind, m].astype(F32) + y_recv[kind, m].astype(F32)).astype(BF16)
        h_buf[m] = (h_buf[m].astype(F32) + total.astype(F32)).astype(BF16)

    def act_copies(t):
        return gather_copies(act_all, t, act_ss, act_rs)

    def out_copy(m, k):
        row = pl.multiple_of(quarter[k] * (NM * R) + m * R, R)
        return pltpu.make_async_copy(h_buf.at[m, pl.ds(k * R, R)], hid_out.at[pl.ds(row, R)], o_sem.at[m, k])

    def mlp_iter(t):
        @pl.when((t >= O2) & (t < n_mlp + O2))
        def _():
            stage2(t - O2)

        @pl.when((t >= O3) & (t < n_mlp + O3))
        def _():
            s = t - O3
            full = stage3(s)
            gate, up = full[:, :CW].astype(F32), full[:, CW:].astype(F32)
            act_all[s, pl.ds(0, R), :] = (jax.nn.silu(gate) * up).astype(BF16)
            to_core, to_chip, _ = act_copies(s)
            to_chip().start()
            to_core().start()

        @pl.when((t >= O4) & (t < n_mlp + O4))
        def _():
            _, to_chip, relay = act_copies(t - O4)
            to_chip().wait_recv()
            relay().start()

        @pl.when(t < n_mlp)
        def _():
            m, j = (0, t) if NM == 1 else (lax.div(t, n_ffn), lax.rem(t, n_ffn))

            @pl.when(t < n_ffn)
            def _():
                for cp in wgu_copy(t):
                    cp.wait()
            stage1(t, m, wgu_buf[j])

        @pl.when((t >= O5) & (t < n_mlp + O5))
        def _():
            s = t - O5
            m, j = (0, s) if NM == 1 else (lax.div(s, n_ffn), lax.rem(s, n_ffn))
            to_core, _, relay = act_copies(s)
            to_core().wait_recv()
            relay().wait_recv()

            @pl.when(s == 0)
            def _():
                wd_copy.wait()
            acc_buf[m] += dot(act_all[s], wd_buf[pl.ds(pl.multiple_of(j * CW, CW), CW), :])

    pl.semaphore_wait(barrier, 4)

    if head:
        for m in range(NM):
            attn_all[m, pl.ds(0, R), :] = attn_in[pl.ds(m * R, R), :]
            to_core, to_chip, _ = attn_copies(m)
            to_chip().start()
            to_core().start()
            acc_buf[m] = jnp.zeros(acc_buf.shape[1:], F32)
        for m in range(NM):
            _, to_chip, relay = attn_copies(m)
            to_chip().wait_recv()
            relay().start()
        for m in range(NM):
            for k in range(4):
                hid_copy(m, k).wait()
        wo_copy.wait()
        for m in range(NM):
            to_core, _, relay = attn_copies(m)
            to_core().wait_recv()
            relay().wait_recv()
            y_start(0, m, dot(attn_all[m], wo_buf[...]))
        for m in range(NM):
            y_finish(0, m)
            stats_start(0, m)
        for m in range(NM):
            norm(0, m, g_mlp[pl.ds(layer, 1), :])

        def body(t, c):
            mlp_iter(t)
            return c
        lax.fori_loop(0, n_mlp + O5, body, 0)
        for m in range(NM):
            y_start(1, m, acc_buf[m])
        for m in range(NM):
            y_finish(1, m)
            if tail:
                stats_start(1, m)
            for k in range(4):
                out_copy(m, k).start()
    else:
        for m in range(NM):
            for k in range(4):
                hid_copy(m, k).wait()
            stats_start(1, m)

    if tail:
        for cp in wqkv_copies:
            cp.wait()
        for m in range(NM):
            norm(1, m, g_attn[pl.ds(tail_layer, 1), :])
        n_all = n_qkv * NM
        for t in range(n_all + 3):
            if 1 <= t < n_all + 1:
                stage2(n_mlp + t - 1)
            if t < n_all:
                stage1(n_mlp + t, t // n_qkv, wqkv_buf[t % n_qkv])
            if t >= 3:
                m, j = divmod(t - 3, n_qkv)
                qkv_out[j, pl.ds(m * R, R), :] = stage3(n_mlp + t - 3)

    def drain(s, c):
        d_copy(s).wait_send()
        x_copy(s).wait_send()
        return c
    lax.fori_loop(0, dsend.shape[0], drain, 0)
    if head:
        def drain_act(s, c):
            for cp in act_copies(s):
                cp().wait_send()
            return c
        lax.fori_loop(0, n_mlp, drain_act, 0)
        for m in range(NM):
            for cp in attn_copies(m):
                cp().wait_send()
            for k in range(4):
                out_copy(m, k).wait()


def chain_call(head, tail, layer, cid, model_dim, hidden, attn=None, g_mlp=None, wo=None, wg=None, wu=None, wd=None, g_attn=None, wq=None, wk=None, wv=None):
    batch, feat = hidden.shape
    M = batch // NM
    R = M // 4
    vmem = pl.BlockSpec(memory_space=pltpu.VMEM)
    hbm = pl.BlockSpec(memory_space=pl.ANY)
    args, in_specs = [hidden], [hbm]
    out_shape, out_specs = [], []
    n_items = 0
    if head:
        args += [attn, g_mlp, wo, wg, wu, wd]
        in_specs += [vmem, vmem, hbm, hbm, hbm, hbm]
        out_shape.append(jax.ShapeDtypeStruct(hidden.shape, hidden.dtype))
        out_specs.append(hbm)
        n_ffn = wg.shape[2] // CW
        n_items += n_ffn * NM
    if tail:
        args += [g_attn, wq, wk, wv]
        in_specs += [vmem, hbm, hbm, hbm]
        out_shape.append(jax.ShapeDtypeStruct((6, batch // 4, IW), BF16))
        out_specs.append(vmem)
        n_items += 6 * NM
    dma = pltpu.SemaphoreType.DMA
    scratch = [
        pltpu.VMEM((NM, M, feat), BF16), pltpu.VMEM((NM, M, feat), BF16), pltpu.VMEM((2, NM, 4, 8, 128), F32),
        pltpu.VMEM((4, 2 * R, IW), F32), pltpu.VMEM((4, R, IW), F32),
        pltpu.VMEM((n_items, 2 * R, IW), BF16), pltpu.VMEM((n_items, 2 * R, IW), BF16),
        pltpu.VMEM((n_items, R, IW), BF16), pltpu.VMEM((n_items, R, IW), BF16),
        dma((NM, 4)), dma((2, NM, 3)), dma((2, NM, 3)), dma((n_items,)), dma((n_items,)), dma((n_items,)), dma((n_items,))]
    if head:
        scratch += [
            pltpu.VMEM((NM, M, attn.shape[1]), BF16), pltpu.VMEM(wo.shape[1:], BF16), pltpu.VMEM((n_ffn, feat, IW), BF16),
            pltpu.VMEM(wd.shape[1:], BF16), pltpu.VMEM((NM, M, feat), F32), pltpu.VMEM((n_ffn * NM, M, CW), BF16),
            pltpu.VMEM((2, NM, M, feat), BF16), pltpu.VMEM((2, NM, M, feat), BF16),
            dma((3, NM)), dma((3, NM)), dma((2, NM)), dma((2, NM)), dma((3, n_ffn * NM)), dma((3, n_ffn * NM)),
            dma, dma((2, n_ffn)), dma, dma((NM, 4))]
    if tail:
        scratch += [pltpu.VMEM((6, feat, IW), BF16), dma((6,))]
    return pl.pallas_call(
        functools.partial(chain_kernel, head, tail, layer, model_dim),
        out_shape=out_shape, in_specs=in_specs, out_specs=out_specs, scratch_shapes=scratch,
        name=f'chain_{int(head)}{int(tail)}',
        compiler_params=pltpu.CompilerParams(collective_id=cid, has_side_effects=True, vmem_limit_bytes=60 * 1024 * 1024),
    )(*args)


def attn_kernel(layer, pos_ref, qkv_ref, cos_ref, sin_ref, qg_ref, kg_ref, k_ref, v_ref, *refs):
    k_out, v_out, o_ref, q_buf, kv_buf, o_buf = refs[-6:]
    step = pl.program_id(0)
    local = o_ref.shape[0]
    n_q = q_buf.shape[0] // local
    n_kv = kv_buf.shape[1] // local
    n_rows = k_ref.shape[2]
    group = n_q // n_kv
    per_chunk = qkv_ref.shape[2] // HEAD_DIM

    def head_of(idx):
        return qkv_ref[idx // per_chunk, :, pl.ds((idx % per_chunk) * HEAD_DIM, HEAD_DIM)].astype(F32)

    @pl.when(step == 0)
    def _():
        cos_tab, sin_tab = cos_ref[...], sin_ref[...]

        def norm_rope(vals, gain):
            normed = vals * lax.rsqrt(jnp.mean(vals * vals, axis=-1, keepdims=True) + NORM_EPS) * gain
            return (normed * cos_tab + pltpu.roll(normed, HEAD_DIM // 2, 1) * sin_tab).astype(BF16).astype(F32)
        for h in range(n_q):
            q_buf[pl.ds(h * local, local), :] = norm_rope(head_of(h), qg_ref[pl.ds(layer, 1), :].astype(F32))
        for h in range(n_kv):
            kv_buf[0, pl.ds(h * local, local), :] = norm_rope(head_of(n_q + h), kg_ref[pl.ds(layer, 1), :].astype(F32))
            kv_buf[1, pl.ds(h * local, local), :] = head_of(n_q + n_kv + h)

    row_ids = lax.broadcasted_iota(jnp.int32, (16, HEAD_DIM), 0)
    lane_ids = lax.broadcasted_iota(jnp.int32, (n_q, n_rows), 1)
    head_hit = lax.rem(lane_ids, n_kv) == lax.div(lax.broadcasted_iota(jnp.int32, (n_q, n_rows), 0), group)
    lane_of = jnp.where(head_hit, lane_ids, n_rows)
    for i in range(SB):
        b = step * SB + i
        pos = pos_ref[b]
        row = pos * n_kv
        base = pl.multiple_of(lax.div(row, 16) * 16, 16)
        hit = lax.div(row_ids, n_kv) == lax.div(row - base, n_kv)
        for src, dst, which in ((k_ref, k_out, 0), (v_ref, v_out, 1)):
            dst[0, i] = src[0, i]
            new = kv_buf[which, pl.ds(b, n_kv, stride=local), :]
            new = jnp.concatenate([new] * (16 // n_kv), axis=0)
            old = src[0, i, pl.ds(base, 16), :]
            dst[0, i, pl.ds(base, 16), :] = jnp.where(hit, new, old.astype(F32)).astype(BF16)
        q = q_buf[pl.ds(b, n_q, stride=local), :].astype(BF16)
        scores = lax.dot_general(q, k_out[0, i], (((1,), (1,)), ((), ())), preferred_element_type=F32) * (HEAD_DIM ** -0.5)
        scores = jnp.where(lane_of < row + n_kv, scores, -1e30)
        e = jnp.exp(scores - jnp.max(scores, axis=-1, keepdims=True))
        probs = (e / jnp.sum(e, axis=-1, keepdims=True)).astype(BF16)
        o_buf[pl.ds(b, n_q, stride=local), :] = dot(probs, v_out[0, i])

    @pl.when(step == pl.num_programs(0) - 1)
    def _():
        for h in range(n_q):
            o_ref[:, pl.ds(h * HEAD_DIM, HEAD_DIM)] = o_buf[pl.ds(h * local, local), :].astype(BF16)


def attn_call(layer, pos, qkv, cos_tab, sin_tab, q_gain, k_gain, k_cache, v_cache, prev):
    layers, local, n_rows, _ = k_cache.shape
    n_kv = 4
    n_q = 16
    smem = pl.BlockSpec(memory_space=pltpu.SMEM)
    vmem = pl.BlockSpec(memory_space=pltpu.VMEM)
    block = pl.BlockSpec((1, SB, n_rows, HEAD_DIM), lambda s: (layer, s, 0, 0))
    args = [pos, qkv, cos_tab, sin_tab, q_gain, k_gain, k_cache, v_cache]
    in_specs = [smem, vmem, vmem, vmem, vmem, vmem, block, block]
    aliases = {}
    if prev is not None:
        args += list(prev)
        in_specs += [pl.BlockSpec(memory_space=pl.ANY)] * 2
        aliases = {8: 0, 9: 1}
    return pl.pallas_call(
        functools.partial(attn_kernel, layer), grid=(local // SB,),
        out_shape=[jax.ShapeDtypeStruct(k_cache.shape, BF16)] * 2 + [jax.ShapeDtypeStruct((local, n_q * HEAD_DIM), BF16)],
        in_specs=in_specs,
        out_specs=[block, block, pl.BlockSpec((local, n_q * HEAD_DIM), lambda s: (0, 0))],
        scratch_shapes=[pltpu.VMEM((n_q * local, HEAD_DIM), F32), pltpu.VMEM((2, n_kv * local, HEAD_DIM), F32), pltpu.VMEM((n_q * local, HEAD_DIM), F32)],
        input_output_aliases=aliases, name=f'attn_{layer}',
        compiler_params=pltpu.CompilerParams(dimension_semantics=('arbitrary',), vmem_limit_bytes=48 * 1024 * 1024),
    )(*args)


def solution(mesh):
    group_size = mesh.shape['x']
    cache_spec = P(None, ('dp', 'x'), None, 'y', None)
    col_spec = P(None, 'x', 'y')
    row_spec = P(None, 'y', 'x')
    in_specs = (P('dp', 'x'), P('dp'), cache_spec, cache_spec, P(None, 'x'), P(None, 'x'), P(), P(), col_spec, col_spec, col_spec, row_spec, col_spec, col_spec, row_spec)
    out_specs = (P('dp', 'x'), cache_spec, cache_spec)

    def device_step(hidden, positions, k_cache, v_cache, g_attn, g_mlp, q_gain, k_gain, w_q, w_k, w_v, w_o, w_gate, w_up, w_down):
        model_dim = hidden.shape[1] * group_size
        layers, local, cache_len, n_kv, _ = k_cache.shape
        my_pos = lax.dynamic_slice_in_dim(positions, lax.axis_index('x') * local, local)
        half = HEAD_DIM // 2
        inv_freq = jnp.power(ROPE_BASE, -2.0 * jnp.arange(half, dtype=F32) / HEAD_DIM)
        angles = my_pos.astype(F32)[:, None] * inv_freq[None, :]
        cos_half, sin_half = jnp.cos(angles), jnp.sin(angles)
        cos_tab = jnp.concatenate([cos_half, cos_half], axis=1)
        sin_tab = jnp.concatenate([-sin_half, sin_half], axis=1)
        k_rows = k_cache.reshape(layers, local, cache_len * n_kv, HEAD_DIM)
        v_rows = v_cache.reshape(layers, local, cache_len * n_kv, HEAD_DIM)
        (qkv,) = chain_call(False, True, 0, 0, model_dim, hidden, g_attn=g_attn, wq=w_q, wk=w_k, wv=w_v)
        k_new, v_new, attn = attn_call(0, my_pos, qkv, cos_tab, sin_tab, q_gain, k_gain, k_rows, v_rows, None)
        hidden, qkv = chain_call(True, True, 0, 1, model_dim, hidden, attn, g_mlp, w_o, w_gate, w_up, w_down, g_attn, w_q, w_k, w_v)
        k_new, v_new, attn = attn_call(1, my_pos, qkv, cos_tab, sin_tab, q_gain, k_gain, k_rows, v_rows, (k_new, v_new))
        (hidden,) = chain_call(True, False, 1, 2, model_dim, hidden, attn, g_mlp, w_o, w_gate, w_up, w_down)
        return hidden, k_new.reshape(k_cache.shape), v_new.reshape(v_cache.shape)

    return jax.shard_map(device_step, mesh=mesh, in_specs=in_specs, out_specs=out_specs, check_vma=False)
```

time: 586 us -> 276 us (0.47); the launches traced: 577 us -> 276 us
  Pallas kernels: 0 us -> 267 us
  waiting for transfers between devices: 267 us -> 0 us
  other arithmetic: 172 us -> 1.05 us
  matrix products: 90 us -> 0 us
  blocking collectives: 29.8 us -> 0 us
  between operations: 15 us -> 0.72 us
    pallas_call x0 -> x5, Pallas kernels: none -> 267 us  [the longest x3 200 us: chain_call(): pl.pallas_call(functools.partial(chain_kernel, head, tail, layer, model_d...]
    psum x6 -> x0, waiting for transfers between devices: 196 us -> none  [the longest x2 140 us: device_step(): lax.psum(jnp.concatenate([jnp.dot(normed_mlp, w_gate[layer_idx], preferre...]
    select_n x3 -> x0, other arithmetic: 95.7 us -> none  [the longest x2 51.9 us: cache_attention(): k_new = jnp.where(slot_hit, k_rot[:, None], k_cache)]
    dot_general x16 -> x0, matrix products: 69 us -> none  [the longest x2 16.4 us: cache_attention(): jnp.einsum('bkgl,blke->bkge', att_probs, v_new, preferred_element_type=jn...]
    another operation x5 -> x0, other arithmetic: 54.4 us -> none  [the longest x1 53.6 us: device_step(): return (hidden, jnp.stack(k_list), jnp.stack(v_list))]
    reduce_scatter x2 -> x0, waiting for transfers between devices: 43.4 us -> none  [device_step(): lax.psum_scatter(proj_parts, 'x', scatter_dimension=0, tiled=True)]
    psum x4 -> x0, blocking collectives: 29.8 us -> none  [sharded_rms(): lax.psum(jnp.sum(hidden_f32 * hidden_f32, axis=1, keepdims=True), 'x')]
    all_gather x2 -> x0, waiting for transfers between devices: 27.7 us -> none  [device_step(): attn_all = lax.all_gather(attn_local, 'x', axis=0, tiled=True)]
  transfers between devices with their start and end apart: 10 -> 0, of which waited for: 9 -> 0; matrix products, arithmetic and copies ran while one was open for 17% -> 0% of each run, Pallas kernels for 0% -> 0%
where the time goes in v1:
time: 276 us
  Pallas kernels  267 us (97%)
  local copies, waits for them, and re-layouts  6.42 us (2%)
    pallas_call x3, Pallas kernels, chain_call(): pl.pallas_call(functools.partial(chain_kernel, head, tail, layer, model_d...  200 us
    pallas_call x2, Pallas kernels, attn_call(): pl.pallas_call(functools.partial(attn_kernel, layer), grid=(local // SB,)...  67.8 us
    unnamed x17, local copies, waits for them, and re-layouts  6.42 us

profile of v1, /device:TPU:0, one launch (start us, length us, event | category | flops | bytes accessed | tf_op | source)
XLA Modules:
  0.0 275.6 jit_solution(5485273607879736210)
XLA Ops:
  0.6 0.8 fusion.1
  1.4 0.2 fusion
  1.6 0.1 pad_maximum_fusion
  1.7 20.5 %chain_01.1.qkv_ref = bf16[6,64,512]{2,1,0:T(8,128)(2,1)} custom-call(bf16[256,640]{1,0:T(8,128)(2,1)} %refs_0_.3, bf16[2,640]{1,0:T(2,128)(2,1)} %refs_7_.1, bf16[2,640,2048]{2,1,0:T(8,128)(2,1)} %refs_8_.1, bf16[2,640,512]{2,1,0:T(8,128)(2,1)} %refs_9_.1, bf16[2,640,512]{2,1,0:T(8,128)(2,1)} %refs_10_.1), custom_call_target="tpu_custom_call" | custom-call | tf_op jit(solution)/shard_map/chain_01/pallas_call | solution.py:343
  22.2 0.0 copy-start
  22.2 1.0 copy-done
  23.2 0.0 copy-start.4
  23.2 0.7 copy-done.4
  23.9 0.0 copy-start.6
  23.9 0.7 copy-done.6
  24.5 33.9 %attn_0.1 = (bf16[2,64,1024,128]{3,2,1,0:T(8,128)(2,1)}, bf16[2,64,1024,128]{3,2,1,0:T(8,128)(2,1)}, bf16[64,2048]{1,0:T(8,128)(2,1)S(1)}) custom-call(s32[64]{0:T(128)S(1)} %get-tuple-element.20.pos_ref, bf16[6,64,512]{2,1,0:T(8,128)(2,1)S(1)} %copy-done, f32[64,128]{1,0:T(8,128)S(1)} %get-tuple-element.24.cos_ref, ...), custom_call_target="tpu_custom_call" | custom-call | tf_op jit(solution)/shard_map/attn_0/pallas_call | solution.py:420
  58.4 0.0 copy-start.3
  58.4 0.7 copy-done.3
  59.1 0.0 copy-start.5
  59.1 0.0 copy-start.7
  59.1 98.3 %chain_11.1 = (bf16[256,640]{1,0:T(8,128)(2,1)}, bf16[6,64,512]{2,1,0:T(8,128)(2,1)}) custom-call(bf16[256,640]{1,0:T(8,128)(2,1)} %refs_0_.3, bf16[64,2048]{1,0:T(8,128)(2,1)} %copy-done.3, bf16[2,640]{1,0:T(2,128)(2,1)} %refs_2_.5, bf16[2,2048,640]{2,1,0:T(8,128)(2,1)} %refs_3_.5, bf16[2,640,4864]{2,1,0:T(8,128)(2,1)} %refs_4_.5, ...), custom_call_target="tpu_custom_call" | custom-call | tf_op jit(solution)/shard_map/chain_11/pallas_call | solution.py:343
  157.4 0.0 copy-done.5
  157.4 0.0 copy-done.7
  157.4 0.0 copy-start.1
  157.4 1.0 copy-done.1
  158.4 33.9 %attn_1.1 = (bf16[2,64,1024,128]{3,2,1,0:T(8,128)(2,1)}, bf16[2,64,1024,128]{3,2,1,0:T(8,128)(2,1)}, bf16[64,2048]{1,0:T(8,128)(2,1)S(1)}) custom-call(s32[64]{0:T(128)S(1)} %get-tuple-element.20.pos_ref, bf16[6,64,512]{2,1,0:T(8,128)(2,1)S(1)} %copy-done.1, f32[64,128]{1,0:T(8,128)S(1)} %get-tuple-element.24.cos_ref, ...), custom_call_target="tpu_custom_call", output_to_operand_aliasing={{0}: (8, {}), {1}: (9, {})} | custom-call | tf_op jit(solution)/shard_map/attn_1/pallas_call | solution.py:420
  192.3 0.0 copy-start.2
  192.3 0.7 copy-done.2
  193.0 80.8 %chain_10.1 = bf16[256,640]{1,0:T(8,128)(2,1)} custom-call(bf16[256,640]{1,0:T(8,128)(2,1)} %get-tuple-element.12.refs_0_, bf16[64,2048]{1,0:T(8,128)(2,1)} %copy-done.2, bf16[2,640]{1,0:T(2,128)(2,1)} %refs_2_.5, bf16[2,2048,640]{2,1,0:T(8,128)(2,1)} %refs_3_.5, bf16[2,640,4864]{2,1,0:T(8,128)(2,1)} %refs_4_.5, bf16[2,640,4864]{2,1,0:T(8,128)(2,1)} %refs_5_.3, ...), custom_call_target="tpu_custom_call" | custom-call | tf_op jit(solution)/shard_map/chain_10/pallas_call | solution.py:343
  273.8 1.7 copy.23
  (1 shorter events, 0.0 us)
Async XLA Ops:
  22.2 1.0 copy-start
  23.2 0.7 copy-start.4
  23.9 0.7 copy-start.6
  58.4 0.7 copy-start.3
  59.1 98.3 %copy-start.5 = (bf16[2,128]{1,0:T(2,128)(2,1)S(1)}, bf16[2,128]{1,0:T(2,128)(2,1)}, u32[]{:S(2)}) copy-start(bf16[2,128]{1,0:T(2,128)(2,1)} %qg_ref.3) | copy-start | bytes 1540
  59.1 98.3 %copy-start.7 = (bf16[2,128]{1,0:T(2,128)(2,1)S(1)}, bf16[2,128]{1,0:T(2,128)(2,1)}, u32[]{:S(2)}) copy-start(bf16[2,128]{1,0:T(2,128)(2,1)} %kg_ref.3) | copy-start | bytes 1540
  157.4 1.0 copy-start.1
  192.3 0.7 copy-start.2

commit v2 on v1

--- a/solution.py
+++ b/solution.py
@@ -14,20 +14,27 @@
 BF16 = jnp.bfloat16
 F32 = jnp.float32
 
-NM = 1
 CW = 256
 IW = 2 * CW
-O2, O3, O4, O5 = 1, 3, 5, 6
+O2, O3, O4, O5 = 2, 5, 8, 10
+E1, E2, E3, E4 = 2, 8, 6, 10
+RING = 8
 SB = 8
+NBUF = 3
 MASK = (0, 2, 1, 3)
 POS = (0, 2, 1, 3)
 
 
+def groups(head):
+    return 2 if head else 1
+
+
 def dot(a, b):
     return jnp.dot(a, b, preferred_element_type=F32)
 
 
-def chain_kernel(head, tail, layer, model_dim, *refs):
+def chain_kernel(head, tail, layer, n_pref, model_dim, *refs):
+    NM = groups(head)
     it = iter(refs)
     hid_in = next(it)
     if head:
@@ -36,18 +43,18 @@
     if tail:
         tail_layer = layer + 1 if head else layer
         g_attn = next(it)
-        wq_in, wk_in, wv_in = (next(it).at[tail_layer] for _ in range(3))
+        wq_in, wk_in, wv_in, k_in, v_in = (next(it).at[tail_layer] for _ in range(5))
     if head:
         hid_out = next(it)
     if tail:
-        qkv_out = next(it)
+        qkv_out, pref_out = next(it), next(it)
     h_buf, n_buf, stat_buf, keep_buf, own_buf, dsend, drecv, xsend, xrecv = (next(it) for _ in range(9))
     h_sem, st_ss, st_rs, d_ss, d_rs, x_ss, x_rs = (next(it) for _ in range(7))
     if head:
         attn_all, wo_buf, wgu_buf, wd_buf, acc_buf, act_all, y_send, y_recv = (next(it) for _ in range(8))
-        ag_ss, ag_rs, y_ss, y_rs, act_ss, act_rs, wo_sem, wgu_sem, wd_sem, o_sem = (next(it) for _ in range(10))
-    if tail:
-        wqkv_buf, wqkv_sem = (next(it) for _ in range(2))
+        ag_ss, ag_rs, y_ss, y_rs, act_ss, act_rs, wo_sem, wgu_sem, wd_sem, o_sem, a_sem = (next(it) for _ in range(11))
+    if tail:
+        wqkv_buf, wqkv_sem, pref_sem = (next(it) for _ in range(3))
 
     me = lax.axis_index('x')
     yy = lax.axis_index('y')
@@ -61,6 +68,15 @@
     n_ffn = act_all.shape[0] // NM if head else 0
     n_mlp = n_ffn * NM
     n_qkv = 6
+    ring = dsend.shape[0]
+    n_items = drecv.shape[0]
+
+    def after_ring(s, action):
+        if isinstance(s, int):
+            if s >= ring:
+                action()
+        else:
+            pl.when(s >= ring)(action)
 
     barrier = pltpu.get_barrier_semaphore()
     for peer in ({'x': d1}, {'x': d2}, {'x': d3}, {'y': 1 - yy}):
@@ -68,6 +84,12 @@
 
     def remote(src, dst, ss, rs, peer):
         return pltpu.make_async_remote_copy(src_ref=src, dst_ref=dst, send_sem=ss, recv_sem=rs, device_id=peer, device_id_type=MESH)
+
+    def attn_own(m):
+        return pltpu.make_async_copy(attn_in.at[pl.ds(m * R, R)], attn_all.at[m, pl.ds(0, R)], a_sem.at[m])
+    if head:
+        for m in range(NM):
+            attn_own(m).start()
 
     def hid_copy(m, k):
         row = pl.multiple_of(quarter[k] * (NM * R) + m * R, R)
@@ -100,6 +122,14 @@
     if tail:
         for cp in wqkv_copies:
             cp.start()
+
+    def pref_copy(blk, c):
+        seqs = pl.ds(blk * SB, SB)
+        return pltpu.make_async_copy((k_in, v_in)[c].at[seqs], pref_out.at[blk, c], pref_sem.at[blk, c])
+    if tail:
+        for blk in range(n_pref):
+            for c in (0, 1):
+                pref_copy(blk, c).start()
 
     def diag():
         return lax.broadcasted_iota(jnp.int32, (R, 128), 0) == lax.broadcasted_iota(jnp.int32, (R, 128), 1)
@@ -129,21 +159,23 @@
             n_buf[m, pl.ds(k * R, R), :] = (hv * lax.rsqrt(col / model_dim + NORM_EPS) * gain_row).astype(BF16)
 
     def d_copy(s):
-        return remote(dsend.at[s], drecv.at[s], d_ss.at[s], d_rs.at[s], {'x': d1})
+        return remote(dsend.at[lax.rem(s, ring)], drecv.at[s], d_ss.at[s], d_rs.at[s], {'x': d1})
 
     def x_copy(s):
-        return remote(xsend.at[s], xrecv.at[s], x_ss.at[s], x_rs.at[s], {'x': d2})
+        return remote(xsend.at[lax.rem(s, ring)], xrecv.at[s], x_ss.at[s], x_rs.at[s], {'x': d2})
 
     def stage1(s, m, w):
         part = dot(n_buf[m], w)
         keep_buf[lax.rem(s, keep_buf.shape[0])] = part[:2 * R]
-        dsend[s] = part[2 * R:].astype(BF16)
+        after_ring(s, lambda: d_copy(s - ring).wait_send())
+        dsend[lax.rem(s, ring)] = part[2 * R:].astype(BF16)
         d_copy(s).start()
 
     def stage2(s):
         d_copy(s).wait_recv()
         slot = lax.rem(s, keep_buf.shape[0])
-        xsend[s] = (keep_buf[slot, pl.ds(R, R), :] + drecv[s, pl.ds(R, R), :].astype(F32)).astype(BF16)
+        after_ring(s, lambda: x_copy(s - ring).wait_send())
+        xsend[lax.rem(s, ring)] = (keep_buf[slot, pl.ds(R, R), :] + drecv[s, pl.ds(R, R), :].astype(F32)).astype(BF16)
         x_copy(s).start()
         own_buf[lax.rem(s, own_buf.shape[0])] = keep_buf[slot, pl.ds(0, R), :] + drecv[s, pl.ds(0, R), :].astype(F32)
 
@@ -178,6 +210,17 @@
     def out_copy(m, k):
         row = pl.multiple_of(quarter[k] * (NM * R) + m * R, R)
         return pltpu.make_async_copy(h_buf.at[m, pl.ds(k * R, R)], hid_out.at[pl.ds(row, R)], o_sem.at[m, k])
+
+    def mid_ready(m):
+        y_finish(0, m)
+        stats_start(0, m)
+
+    def layer_done(m):
+        y_finish(1, m)
+        if tail:
+            stats_start(1, m)
+        for k in range(4):
+            out_copy(m, k).start()
 
     def mlp_iter(t):
         @pl.when((t >= O2) & (t < n_mlp + O2))
@@ -227,7 +270,7 @@
 
     if head:
         for m in range(NM):
-            attn_all[m, pl.ds(0, R), :] = attn_in[pl.ds(m * R, R), :]
+            attn_own(m).wait()
             to_core, to_chip, _ = attn_copies(m)
             to_chip().start()
             to_core().start()
@@ -245,24 +288,26 @@
             to_core().wait_recv()
             relay().wait_recv()
             y_start(0, m, dot(attn_all[m], wo_buf[...]))
-        for m in range(NM):
-            y_finish(0, m)
-            stats_start(0, m)
-        for m in range(NM):
-            norm(0, m, g_mlp[pl.ds(layer, 1), :])
+        y_finish(0, 0)
+        stats_start(0, 0)
+        norm(0, 0, g_mlp[pl.ds(layer, 1), :])
+        events = {}
+        if NM == 2:
+            first_done = n_ffn - 1 + O5
+            events = {E1: lambda: mid_ready(1), E2: lambda: norm(0, 1, g_mlp[pl.ds(layer, 1), :]),
+                      first_done: lambda: y_start(1, 0, acc_buf[0]), first_done + E3: lambda: layer_done(0)}
+            if tail:
+                events[first_done + E4] = lambda: norm(1, 0, g_attn[pl.ds(tail_layer, 1), :])
 
         def body(t, c):
             mlp_iter(t)
+            for at, event in events.items():
+                pl.when(t == at)(event)
             return c
         lax.fori_loop(0, n_mlp + O5, body, 0)
-        for m in range(NM):
-            y_start(1, m, acc_buf[m])
-        for m in range(NM):
-            y_finish(1, m)
-            if tail:
-                stats_start(1, m)
-            for k in range(4):
-                out_copy(m, k).start()
+        y_start(1, NM - 1, acc_buf[NM - 1])
+        if not (tail and NM == 2):
+            layer_done(NM - 1)
     else:
         for m in range(NM):
             for k in range(4):
@@ -272,23 +317,32 @@
     if tail:
         for cp in wqkv_copies:
             cp.wait()
-        for m in range(NM):
-            norm(1, m, g_attn[pl.ds(tail_layer, 1), :])
         n_all = n_qkv * NM
+        if not (head and NM == 2):
+            for m in range(NM):
+                norm(1, m, g_attn[pl.ds(tail_layer, 1), :])
         for t in range(n_all + 3):
             if 1 <= t < n_all + 1:
                 stage2(n_mlp + t - 1)
+            if head and NM == 2 and t == n_qkv:
+                layer_done(1)
+                norm(1, 1, g_attn[pl.ds(tail_layer, 1), :])
             if t < n_all:
                 stage1(n_mlp + t, t // n_qkv, wqkv_buf[t % n_qkv])
             if t >= 3:
                 m, j = divmod(t - 3, n_qkv)
                 qkv_out[j, pl.ds(m * R, R), :] = stage3(n_mlp + t - 3)
 
+    if tail:
+        for blk in range(n_pref):
+            for c in (0, 1):
+                pref_copy(blk, c).wait()
+
     def drain(s, c):
         d_copy(s).wait_send()
         x_copy(s).wait_send()
         return c
-    lax.fori_loop(0, dsend.shape[0], drain, 0)
+    lax.fori_loop(max(n_items - ring, 0), n_items, drain, 0)
     if head:
         def drain_act(s, c):
             for cp in act_copies(s):
@@ -302,34 +356,37 @@
                 out_copy(m, k).wait()
 
 
-def chain_call(head, tail, layer, cid, model_dim, hidden, attn=None, g_mlp=None, wo=None, wg=None, wu=None, wd=None, g_attn=None, wq=None, wk=None, wv=None):
+def chain_call(head, tail, layer, cid, n_pref, vmem_mib, model_dim, hidden, attn=None, g_mlp=None, wo=None, wg=None, wu=None, wd=None, g_attn=None, wq=None, wk=None, wv=None, k_rows=None, v_rows=None):
     batch, feat = hidden.shape
+    NM = groups(head)
     M = batch // NM
     R = M // 4
     vmem = pl.BlockSpec(memory_space=pltpu.VMEM)
-    hbm = pl.BlockSpec(memory_space=pl.ANY)
+    hbm = pl.BlockSpec(memory_space=pltpu.HBM)
     args, in_specs = [hidden], [hbm]
     out_shape, out_specs = [], []
     n_items = 0
     if head:
         args += [attn, g_mlp, wo, wg, wu, wd]
-        in_specs += [vmem, vmem, hbm, hbm, hbm, hbm]
+        in_specs += [hbm, vmem, hbm, hbm, hbm, hbm]
         out_shape.append(jax.ShapeDtypeStruct(hidden.shape, hidden.dtype))
         out_specs.append(hbm)
         n_ffn = wg.shape[2] // CW
         n_items += n_ffn * NM
     if tail:
-        args += [g_attn, wq, wk, wv]
-        in_specs += [vmem, hbm, hbm, hbm]
+        args += [g_attn, wq, wk, wv, k_rows, v_rows]
+        in_specs += [vmem] + [hbm] * 5
         out_shape.append(jax.ShapeDtypeStruct((6, batch // 4, IW), BF16))
+        out_specs.append(vmem)
+        out_shape.append(pltpu.VMEM((n_pref, 2, SB) + k_rows.shape[2:], BF16))
         out_specs.append(vmem)
         n_items += 6 * NM
     dma = pltpu.SemaphoreType.DMA
     scratch = [
         pltpu.VMEM((NM, M, feat), BF16), pltpu.VMEM((NM, M, feat), BF16), pltpu.VMEM((2, NM, 4, 8, 128), F32),
-        pltpu.VMEM((4, 2 * R, IW), F32), pltpu.VMEM((4, R, IW), F32),
-        pltpu.VMEM((n_items, 2 * R, IW), BF16), pltpu.VMEM((n_items, 2 * R, IW), BF16),
-        pltpu.VMEM((n_items, R, IW), BF16), pltpu.VMEM((n_items, R, IW), BF16),
+        pltpu.VMEM((O2 + 1, 2 * R, IW), F32), pltpu.VMEM((O3 - O2 + 1, R, IW), F32),
+        pltpu.VMEM((RING, 2 * R, IW), BF16), pltpu.VMEM((n_items, 2 * R, IW), BF16),
+        pltpu.VMEM((RING, R, IW), BF16), pltpu.VMEM((n_items, R, IW), BF16),
         dma((NM, 4)), dma((2, NM, 3)), dma((2, NM, 3)), dma((n_items,)), dma((n_items,)), dma((n_items,)), dma((n_items,))]
     if head:
         scratch += [
@@ -337,94 +394,145 @@
             pltpu.VMEM(wd.shape[1:], BF16), pltpu.VMEM((NM, M, feat), F32), pltpu.VMEM((n_ffn * NM, M, CW), BF16),
             pltpu.VMEM((2, NM, M, feat), BF16), pltpu.VMEM((2, NM, M, feat), BF16),
             dma((3, NM)), dma((3, NM)), dma((2, NM)), dma((2, NM)), dma((3, n_ffn * NM)), dma((3, n_ffn * NM)),
-            dma, dma((2, n_ffn)), dma, dma((NM, 4))]
-    if tail:
-        scratch += [pltpu.VMEM((6, feat, IW), BF16), dma((6,))]
+            dma, dma((2, n_ffn)), dma, dma((NM, 4)), dma((NM,))]
+    if tail:
+        scratch += [pltpu.VMEM((6, feat, IW), BF16), dma((6,)), dma((n_pref, 2))]
     return pl.pallas_call(
-        functools.partial(chain_kernel, head, tail, layer, model_dim),
+        functools.partial(chain_kernel, head, tail, layer, n_pref, model_dim),
         out_shape=out_shape, in_specs=in_specs, out_specs=out_specs, scratch_shapes=scratch,
         name=f'chain_{int(head)}{int(tail)}',
-        compiler_params=pltpu.CompilerParams(collective_id=cid, has_side_effects=True, vmem_limit_bytes=60 * 1024 * 1024),
+        compiler_params=pltpu.CompilerParams(collective_id=cid, has_side_effects=True, vmem_limit_bytes=vmem_mib * 1024 * 1024),
     )(*args)
 
 
-def attn_kernel(layer, pos_ref, qkv_ref, cos_ref, sin_ref, qg_ref, kg_ref, k_ref, v_ref, *refs):
-    k_out, v_out, o_ref, q_buf, kv_buf, o_buf = refs[-6:]
-    step = pl.program_id(0)
+def attn_kernel(layer, n_pref, pos_ref, qkv_hbm, tabs_hbm, k_hbm, v_hbm, *refs):
+    k_out, v_out, o_ref, pref, kv_slots, q_buf, kv_buf, o_buf, s_buf, p_buf, qkv_ref, tabs_ref, in_sem, out_sem, small_sem = refs[-15:]
+    small = (pltpu.make_async_copy(qkv_hbm, qkv_ref, small_sem.at[0]), pltpu.make_async_copy(tabs_hbm, tabs_ref, small_sem.at[1]))
+    for cp in small:
+        cp.start()
     local = o_ref.shape[0]
     n_q = q_buf.shape[0] // local
     n_kv = kv_buf.shape[1] // local
-    n_rows = k_ref.shape[2]
+    n_rows = k_hbm.shape[2]
     group = n_q // n_kv
     per_chunk = qkv_ref.shape[2] // HEAD_DIM
+    n_blocks = local // SB
+
+    def held(blk, early):
+        return pref.at[blk] if early else kv_slots.at[lax.rem(blk - n_pref, NBUF)]
+
+    def run(blk, early, out, wait):
+        seqs = pl.ds(blk * SB, SB)
+        for c in (0, 1):
+            here = held(blk, early).at[c]
+            if out:
+                cp = pltpu.make_async_copy(here, (k_out, v_out)[c].at[layer, seqs], out_sem.at[blk, c])
+            else:
+                cp = pltpu.make_async_copy((k_hbm, v_hbm)[c].at[layer, seqs], here, in_sem.at[blk, c])
+            cp.wait() if wait else cp.start()
+
+    for blk in range(n_pref, min(n_pref + NBUF, n_blocks)):
+        run(blk, False, False, False)
 
     def head_of(idx):
         return qkv_ref[idx // per_chunk, :, pl.ds((idx % per_chunk) * HEAD_DIM, HEAD_DIM)].astype(F32)
 
-    @pl.when(step == 0)
-    def _():
-        cos_tab, sin_tab = cos_ref[...], sin_ref[...]
-
-        def norm_rope(vals, gain):
-            normed = vals * lax.rsqrt(jnp.mean(vals * vals, axis=-1, keepdims=True) + NORM_EPS) * gain
-            return (normed * cos_tab + pltpu.roll(normed, HEAD_DIM // 2, 1) * sin_tab).astype(BF16).astype(F32)
-        for h in range(n_q):
-            q_buf[pl.ds(h * local, local), :] = norm_rope(head_of(h), qg_ref[pl.ds(layer, 1), :].astype(F32))
-        for h in range(n_kv):
-            kv_buf[0, pl.ds(h * local, local), :] = norm_rope(head_of(n_q + h), kg_ref[pl.ds(layer, 1), :].astype(F32))
-            kv_buf[1, pl.ds(h * local, local), :] = head_of(n_q + n_kv + h)
+    for cp in small:
+        cp.wait()
+    cos_tab, sin_tab = tabs_ref[pl.ds(0, local), :], tabs_ref[pl.ds(local, local), :]
+    gains = [tabs_ref[pl.ds(2 * local + 2 * layer + i, 1), :] for i in (0, 1)]
+
+    def norm_rope(vals, gain):
+        normed = vals * lax.rsqrt(jnp.mean(vals * vals, axis=-1, keepdims=True) + NORM_EPS) * gain
+        return (normed * cos_tab + pltpu.roll(normed, HEAD_DIM // 2, 1) * sin_tab).astype(BF16).astype(F32)
+    for h in range(n_q):
+        q_buf[pl.ds(h * local, local), :] = norm_rope(head_of(h), gains[0])
+    for h in range(n_kv):
+        kv_buf[0, pl.ds(h * local, local), :] = norm_rope(head_of(n_q + h), gains[1])
+        kv_buf[1, pl.ds(h * local, local), :] = head_of(n_q + n_kv + h)
 
     row_ids = lax.broadcasted_iota(jnp.int32, (16, HEAD_DIM), 0)
     lane_ids = lax.broadcasted_iota(jnp.int32, (n_q, n_rows), 1)
     head_hit = lax.rem(lane_ids, n_kv) == lax.div(lax.broadcasted_iota(jnp.int32, (n_q, n_rows), 0), group)
     lane_of = jnp.where(head_hit, lane_ids, n_rows)
-    for i in range(SB):
-        b = step * SB + i
-        pos = pos_ref[b]
-        row = pos * n_kv
-        base = pl.multiple_of(lax.div(row, 16) * 16, 16)
-        hit = lax.div(row_ids, n_kv) == lax.div(row - base, n_kv)
-        for src, dst, which in ((k_ref, k_out, 0), (v_ref, v_out, 1)):
-            dst[0, i] = src[0, i]
-            new = kv_buf[which, pl.ds(b, n_kv, stride=local), :]
-            new = jnp.concatenate([new] * (16 // n_kv), axis=0)
-            old = src[0, i, pl.ds(base, 16), :]
-            dst[0, i, pl.ds(base, 16), :] = jnp.where(hit, new, old.astype(F32)).astype(BF16)
-        q = q_buf[pl.ds(b, n_q, stride=local), :].astype(BF16)
-        scores = lax.dot_general(q, k_out[0, i], (((1,), (1,)), ((), ())), preferred_element_type=F32) * (HEAD_DIM ** -0.5)
-        scores = jnp.where(lane_of < row + n_kv, scores, -1e30)
-        e = jnp.exp(scores - jnp.max(scores, axis=-1, keepdims=True))
-        probs = (e / jnp.sum(e, axis=-1, keepdims=True)).astype(BF16)
-        o_buf[pl.ds(b, n_q, stride=local), :] = dot(probs, v_out[0, i])
-
-    @pl.when(step == pl.num_programs(0) - 1)
-    def _():
-        for h in range(n_q):
-            o_ref[:, pl.ds(h * HEAD_DIM, HEAD_DIM)] = o_buf[pl.ds(h * local, local), :].astype(BF16)
-
-
-def attn_call(layer, pos, qkv, cos_tab, sin_tab, q_gain, k_gain, k_cache, v_cache, prev):
+
+    def block_step(blk, early):
+        ref = held(blk, early)
+        if not early:
+            run(blk, False, False, True)
+        for i in range(SB):
+            b = blk * SB + i
+            row = pos_ref[b] * n_kv
+            base = pl.multiple_of(lax.div(row, 16) * 16, 16)
+            hit = lax.div(row_ids, n_kv) == lax.div(row - base, n_kv)
+            for c in (0, 1):
+                new = kv_buf[c, pl.ds(b, n_kv, stride=local), :]
+                new = jnp.concatenate([new] * (16 // n_kv), axis=0)
+                old = ref[c, i, pl.ds(base, 16), :]
+                ref[c, i, pl.ds(base, 16), :] = jnp.where(hit, new, old.astype(F32)).astype(BF16)
+        for i in range(SB):
+            q = q_buf[pl.ds(blk * SB + i, n_q, stride=local), :].astype(BF16)
+            s_buf[i] = lax.dot_general(q, ref[0, i], (((1,), (1,)), ((), ())), preferred_element_type=F32)
+        run(blk, early, True, False)
+        for i in range(SB):
+            row = pos_ref[blk * SB + i] * n_kv
+            scores = jnp.where(lane_of < row + n_kv, s_buf[i] * (HEAD_DIM ** -0.5), -1e30)
+            e = jnp.exp(scores - jnp.max(scores, axis=-1, keepdims=True))
+            p_buf[i] = (e / jnp.sum(e, axis=-1, keepdims=True)).astype(BF16)
+        for i in range(SB):
+            o_buf[pl.ds(blk * SB + i, n_q, stride=local), :] = dot(p_buf[i], ref[1, i])
+
+    def early_step(blk, carry):
+        block_step(blk, True)
+        return carry
+
+    def late_step(blk, carry):
+        block_step(blk, False)
+
+        @pl.when((blk > n_pref) & (blk - 1 + NBUF < n_blocks))
+        def _():
+            run(blk - 1, False, True, True)
+            run(blk - 1 + NBUF, False, False, False)
+        return carry
+    lax.fori_loop(0, n_pref, early_step, 0)
+    if n_pref < n_blocks:
+        lax.fori_loop(n_pref, n_blocks, late_step, 0)
+
+    for h in range(n_q):
+        o_ref[:, pl.ds(h * HEAD_DIM, HEAD_DIM)] = o_buf[pl.ds(h * local, local), :].astype(BF16)
+    for blk in range(n_pref):
+        run(blk, True, True, True)
+    for blk in range(max(n_blocks - NBUF, n_pref), n_blocks):
+        run(blk, False, True, True)
+
+
+def attn_call(layer, pos, qkv, tabs, k_cache, v_cache, pref, prev):
     layers, local, n_rows, _ = k_cache.shape
     n_kv = 4
     n_q = 16
     smem = pl.BlockSpec(memory_space=pltpu.SMEM)
     vmem = pl.BlockSpec(memory_space=pltpu.VMEM)
-    block = pl.BlockSpec((1, SB, n_rows, HEAD_DIM), lambda s: (layer, s, 0, 0))
-    args = [pos, qkv, cos_tab, sin_tab, q_gain, k_gain, k_cache, v_cache]
-    in_specs = [smem, vmem, vmem, vmem, vmem, vmem, block, block]
-    aliases = {}
+    hbm = pl.BlockSpec(memory_space=pltpu.HBM)
+    args = [pos, qkv, tabs, k_cache, v_cache, pref]
+    in_specs = [smem, hbm, hbm, hbm, hbm, vmem]
+    aliases = {5: 3}
+    n_pref, n_blocks = pref.shape[0], local // SB
     if prev is not None:
         args += list(prev)
-        in_specs += [pl.BlockSpec(memory_space=pl.ANY)] * 2
-        aliases = {8: 0, 9: 1}
+        in_specs += [hbm] * 2
+        aliases.update({6: 0, 7: 1})
     return pl.pallas_call(
-        functools.partial(attn_kernel, layer), grid=(local // SB,),
-        out_shape=[jax.ShapeDtypeStruct(k_cache.shape, BF16)] * 2 + [jax.ShapeDtypeStruct((local, n_q * HEAD_DIM), BF16)],
+        functools.partial(attn_kernel, layer, n_pref),
+        out_shape=[jax.ShapeDtypeStruct(k_cache.shape, BF16)] * 2 + [jax.ShapeDtypeStruct((local, n_q * HEAD_DIM), BF16), jax.ShapeDtypeStruct(pref.shape, BF16)],
         in_specs=in_specs,
-        out_specs=[block, block, pl.BlockSpec((local, n_q * HEAD_DIM), lambda s: (0, 0))],
-        scratch_shapes=[pltpu.VMEM((n_q * local, HEAD_DIM), F32), pltpu.VMEM((2, n_kv * local, HEAD_DIM), F32), pltpu.VMEM((n_q * local, HEAD_DIM), F32)],
+        out_specs=[hbm, hbm, vmem, vmem],
+        scratch_shapes=[pltpu.VMEM((min(NBUF, max(n_blocks - n_pref, 1)) if n_pref < n_blocks else 1, 2, SB if n_pref < n_blocks else 1, n_rows, HEAD_DIM), BF16),
+                        pltpu.VMEM((n_q * local, HEAD_DIM), F32), pltpu.VMEM((2, n_kv * local, HEAD_DIM), F32), pltpu.VMEM((n_q * local, HEAD_DIM), F32),
+                        pltpu.VMEM((SB, n_q, n_rows), F32), pltpu.VMEM((SB, n_q, n_rows), BF16),
+                        pltpu.VMEM(qkv.shape, BF16), pltpu.VMEM(tabs.shape, F32),
+                        pltpu.SemaphoreType.DMA((n_blocks, 2)), pltpu.SemaphoreType.DMA((n_blocks, 2)), pltpu.SemaphoreType.DMA((2,))],
         input_output_aliases=aliases, name=f'attn_{layer}',
-        compiler_params=pltpu.CompilerParams(dimension_semantics=('arbitrary',), vmem_limit_bytes=48 * 1024 * 1024),
+        compiler_params=pltpu.CompilerParams(vmem_limit_bytes=(20 if n_pref == n_blocks else 22) * 1024 * 1024),
     )(*args)
 
 
@@ -444,15 +552,18 @@
         inv_freq = jnp.power(ROPE_BASE, -2.0 * jnp.arange(half, dtype=F32) / HEAD_DIM)
         angles = my_pos.astype(F32)[:, None] * inv_freq[None, :]
         cos_half, sin_half = jnp.cos(angles), jnp.sin(angles)
-        cos_tab = jnp.concatenate([cos_half, cos_half], axis=1)
-        sin_tab = jnp.concatenate([-sin_half, sin_half], axis=1)
+        gains = jnp.stack([q_gain[0], k_gain[0], q_gain[1], k_gain[1]]).astype(F32)
+        tabs = jnp.concatenate([jnp.concatenate([cos_half, cos_half], axis=1), jnp.concatenate([-sin_half, sin_half], axis=1), gains, jnp.zeros((4, HEAD_DIM), F32)])
+        tabs, my_pos, hidden = lax.optimization_barrier((tabs, my_pos, hidden))
         k_rows = k_cache.reshape(layers, local, cache_len * n_kv, HEAD_DIM)
         v_rows = v_cache.reshape(layers, local, cache_len * n_kv, HEAD_DIM)
-        (qkv,) = chain_call(False, True, 0, 0, model_dim, hidden, g_attn=g_attn, wq=w_q, wk=w_k, wv=w_v)
-        k_new, v_new, attn = attn_call(0, my_pos, qkv, cos_tab, sin_tab, q_gain, k_gain, k_rows, v_rows, None)
-        hidden, qkv = chain_call(True, True, 0, 1, model_dim, hidden, attn, g_mlp, w_o, w_gate, w_up, w_down, g_attn, w_q, w_k, w_v)
-        k_new, v_new, attn = attn_call(1, my_pos, qkv, cos_tab, sin_tab, q_gain, k_gain, k_rows, v_rows, (k_new, v_new))
-        (hidden,) = chain_call(True, False, 1, 2, model_dim, hidden, attn, g_mlp, w_o, w_gate, w_up, w_down)
+        attn_tabs = (tabs, k_rows, v_rows)
+        caches = {'k_rows': k_rows, 'v_rows': v_rows}
+        qkv, pref = chain_call(False, True, 0, 0, 8, 16, model_dim, hidden, g_attn=g_attn, wq=w_q, wk=w_k, wv=w_v, **caches)
+        k_new, v_new, attn, _ = attn_call(0, my_pos, qkv, *attn_tabs, pref, None)
+        hidden, qkv, pref = chain_call(True, True, 0, 1, 5, 40, model_dim, hidden, attn, g_mlp, w_o, w_gate, w_up, w_down, g_attn, w_q, w_k, w_v, **caches)
+        k_new, v_new, attn, _ = attn_call(1, my_pos, qkv, *attn_tabs, pref, (k_new, v_new))
+        (hidden,) = chain_call(True, False, 1, 2, 0, 60, model_dim, hidden, attn, g_mlp, w_o, w_gate, w_up, w_down)
         return hidden, k_new.reshape(k_cache.shape), v_new.reshape(v_cache.shape)
 
     return jax.shard_map(device_step, mesh=mesh, in_specs=in_specs, out_specs=out_specs, check_vma=False)

time: 276 us -> 230 us (0.83)
  Pallas kernels: 267 us -> 218 us
  local copies, waits for them, and re-layouts: 6.42 us -> 9.21 us
    pallas_call x5, Pallas kernels: 267 us -> 218 us  [the longest x3 189 us: chain_call(): pl.pallas_call(functools.partial(chain_kernel, head, tail, layer, n_pref,...]
    unnamed x17 -> x15, local copies, waits for them, and re-layouts: 6.42 us -> 8.39 us
where the time goes in v2:
time: 230 us; the launch traced here: 229 us
  Pallas kernels  218 us (95%)
  local copies, waits for them, and re-layouts  9.21 us (4%)
    pallas_call x3, Pallas kernels, chain_call(): pl.pallas_call(functools.partial(chain_kernel, head, tail, layer, n_pref,...  189 us
    pallas_call x2, Pallas kernels, attn_call(): pl.pallas_call(functools.partial(attn_kernel, layer, n_pref), out_shape=[...  29.5 us
    unnamed x15, local copies, waits for them, and re-layouts  8.39 us

profile of v2, /device:TPU:0, one launch (start us, length us, event | category | flops | bytes accessed | tf_op | source)
XLA Modules:
  0.0 229.2 jit_solution(11415828336410117225)
XLA Ops:
  0.6 0.1 pad.5.clone
  0.7 0.8 fusion.1
  1.5 0.7 fusion.2
  2.2 0.2 multiply_cosine_fusion
  2.4 0.1 maximum_maximum_fusion.tabs_hbm
  2.6 0.0 copy-start
  2.6 1.3 copy-done
  3.9 0.0 copy-start.1
  3.9 1.3 copy-done.1
  5.2 0.0 copy-start.2
  5.2 1.0 copy-done.2
  6.2 0.0 copy-start.6
  6.2 0.7 copy-done.6
  6.8 19.1 %chain_01.1 = (bf16[6,64,512]{2,1,0:T(8,128)(2,1)S(1)}, bf16[8,2,8,1024,128]{4,3,2,1,0:T(8,128)(2,1)S(1)}) custom-call(bf16[256,640]{1,0:T(8,128)(2,1)S(1)} %copy-done.2, bf16[2,640]{1,0:T(2,128)(2,1)S(1)} %copy-done.6, bf16[2,640,2048]{2,1,0:T(8,128)(2,1)} %refs_8_.1, bf16[2,640,512]{2,1,0:T(8,128)(2,1)S(1)} %copy-done, bf16[2,640,512]{2,1,0:T(8,128)(2,1)S(1)} %copy-done.1, ...), custom_call_target="tpu_custom_call" | custom-call | tf_op jit(solution)/shard_map/chain_01/pallas_call | solution.py:400
  26.0 14.3 %attn_0.1 = (bf16[2,64,1024,128]{3,2,1,0:T(8,128)(2,1)}, bf16[2,64,1024,128]{3,2,1,0:T(8,128)(2,1)}, bf16[64,2048]{1,0:T(8,128)(2,1)S(1)}, bf16[8,2,8,1024,128]{4,3,2,1,0:T(8,128)(2,1)S(1)}) custom-call(s32[64]{0:T(128)S(1)} %get-tuple-element.18.pos_ref, bf16[6,64,512]{2,1,0:T(8,128)(2,1)S(1)} %get-tuple-element.19.qkv_hbm, ...), custom_call_target="tpu_custom_call", output_to_operand_aliasing={{3}: (5, {})} | custom-call | tf_op jit(solution)/shard_map/attn_0/pallas_call | solution.py:524
  40.3 0.0 copy-start.5
  40.3 0.7 copy-done.5
  41.0 93.5 %chain_11.1 = (bf16[256,640]{1,0:T(8,128)(2,1)}, bf16[6,64,512]{2,1,0:T(8,128)(2,1)}, bf16[5,2,8,1024,128]{4,3,2,1,0:T(8,128)(2,1)S(1)}) custom-call(bf16[256,640]{1,0:T(8,128)(2,1)} %refs_0_.1, bf16[64,2048]{1,0:T(8,128)(2,1)} %copy-done.5, bf16[2,640]{1,0:T(2,128)(2,1)} %refs_2_.5, bf16[2,2048,640]{2,1,0:T(8,128)(2,1)} %refs_3_.5, ...), custom_call_target="tpu_custom_call" | custom-call | tf_op jit(solution)/shard_map/chain_11/pallas_call | solution.py:400
  134.5 0.0 copy-start.3
  134.5 1.0 copy-done.3
  135.5 15.3 %attn_1.1 = (bf16[2,64,1024,128]{3,2,1,0:T(8,128)(2,1)}, bf16[2,64,1024,128]{3,2,1,0:T(8,128)(2,1)}, bf16[64,2048]{1,0:T(8,128)(2,1)S(1)}, bf16[5,2,8,1024,128]{4,3,2,1,0:T(8,128)(2,1)S(1)}) custom-call(s32[64]{0:T(128)S(1)} %get-tuple-element.18.pos_ref, ...), custom_call_target="tpu_custom_call", output_to_operand_aliasing={{3}: (5, {}), {0}: (6, {}), {1}: (7, {})} | custom-call | tf_op jit(solution)/shard_map/attn_1/pallas_call | solution.py:524
  150.8 0.0 copy-start.4
  150.8 0.7 copy-done.4
  151.5 76.0 %chain_10.1 = bf16[256,640]{1,0:T(8,128)(2,1)} custom-call(bf16[256,640]{1,0:T(8,128)(2,1)} %get-tuple-element.23.refs_0_, bf16[64,2048]{1,0:T(8,128)(2,1)} %copy-done.4, bf16[2,640]{1,0:T(2,128)(2,1)} %refs_2_.5, bf16[2,2048,640]{2,1,0:T(8,128)(2,1)} %refs_3_.5, bf16[2,640,4864]{2,1,0:T(8,128)(2,1)} %refs_4_.5, bf16[2,640,4864]{2,1,0:T(8,128)(2,1)} %refs_5_.3, ...), custom_call_target="tpu_custom_call" | custom-call | tf_op jit(solution)/shard_map/chain_10/pallas_call | solution.py:400
  227.5 1.7 copy.27
  (3 shorter events, 0.0 us)
Async XLA Ops:
  2.6 1.3 copy-start
  3.9 1.3 copy-start.1
  5.2 1.0 copy-start.2
  6.2 0.7 copy-start.6
  40.3 0.7 copy-start.5
  134.5 1.0 copy-start.3
  150.8 0.7 copy-start.4

commit v3 on v2

--- a/solution.py
+++ b/solution.py
@@ -16,13 +16,14 @@
 
 CW = 256
 IW = 2 * CW
-O2, O3, O4, O5 = 2, 5, 8, 10
+O2, O3, O4, O5 = 3, 8, 13, 16
 E1, E2, E3, E4 = 2, 8, 6, 10
 RING = 8
 SB = 8
 NBUF = 3
 MASK = (0, 2, 1, 3)
 POS = (0, 2, 1, 3)
+HALVES = ((0, 2), (1, 3))
 
 
 def groups(head):
@@ -164,24 +165,36 @@
     def x_copy(s):
         return remote(xsend.at[lax.rem(s, ring)], xrecv.at[s], x_ss.at[s], x_rs.at[s], {'x': d2})
 
-    def stage1(s, m, w):
+    def stage1_math(s, m, w):
         part = dot(n_buf[m], w)
         keep_buf[lax.rem(s, keep_buf.shape[0])] = part[:2 * R]
+        dsend[lax.rem(s, ring)] = part[2 * R:].astype(BF16)
+
+    def stage1(s, m, w):
         after_ring(s, lambda: d_copy(s - ring).wait_send())
-        dsend[lax.rem(s, ring)] = part[2 * R:].astype(BF16)
+        stage1_math(s, m, w)
         d_copy(s).start()
 
+    def stage2_wait(s):
+        d_copy(s).wait_recv()
+        after_ring(s, lambda: x_copy(s - ring).wait_send())
+
+    def stage2_math(s):
+        slot = lax.rem(s, keep_buf.shape[0])
+        xsend[lax.rem(s, ring)] = (keep_buf[slot, pl.ds(R, R), :] + drecv[s, pl.ds(R, R), :].astype(F32)).astype(BF16)
+        own_buf[lax.rem(s, own_buf.shape[0])] = keep_buf[slot, pl.ds(0, R), :] + drecv[s, pl.ds(0, R), :].astype(F32)
+
     def stage2(s):
-        d_copy(s).wait_recv()
-        slot = lax.rem(s, keep_buf.shape[0])
-        after_ring(s, lambda: x_copy(s - ring).wait_send())
-        xsend[lax.rem(s, ring)] = (keep_buf[slot, pl.ds(R, R), :] + drecv[s, pl.ds(R, R), :].astype(F32)).astype(BF16)
+        stage2_wait(s)
+        stage2_math(s)
         x_copy(s).start()
-        own_buf[lax.rem(s, own_buf.shape[0])] = keep_buf[slot, pl.ds(0, R), :] + drecv[s, pl.ds(0, R), :].astype(F32)
+
+    def stage3_sum(s):
+        return (own_buf[lax.rem(s, own_buf.shape[0])] + xrecv[s].astype(F32)).astype(BF16)
 
     def stage3(s):
         x_copy(s).wait_recv()
-        return (own_buf[lax.rem(s, own_buf.shape[0])] + xrecv[s].astype(F32)).astype(BF16)
+        return stage3_sum(s)
 
     def gather_copies(buf, i, ss, rs):
         own, other = buf.at[i, pl.ds(0, R)], buf.at[i, pl.ds(R, R)]
@@ -192,17 +205,34 @@
     def attn_copies(m):
         return gather_copies(attn_all, m, ag_ss, ag_rs)
 
-    def y_copy(kind, m):
-        return remote(y_send.at[kind, m], y_recv.at[kind, m], y_ss.at[kind, m], y_rs.at[kind, m], {'y': 1 - yy})
-
-    def y_start(kind, m, value):
-        y_send[kind, m] = value.astype(BF16)
-        y_copy(kind, m).start()
-
-    def y_finish(kind, m):
-        y_copy(kind, m).wait()
-        total = (y_send[kind, m].astype(F32) + y_recv[kind, m].astype(F32)).astype(BF16)
-        h_buf[m] = (h_buf[m].astype(F32) + total.astype(F32)).astype(BF16)
+    def y_copy(kind, m, half):
+        rows = pl.ds(half * 2 * R, 2 * R)
+        return remote(y_send.at[kind, m, rows], y_recv.at[kind, m, rows], y_ss.at[kind, m, half], y_rs.at[kind, m, half], {'y': 1 - yy})
+
+    def attn_half(m, half):
+        rows = jnp.concatenate([attn_all[m, pl.ds(k * R, R), :] for k in HALVES[half]], axis=0)
+        y_send[0, m, pl.ds(half * 2 * R, 2 * R), :] = dot(rows, wo_buf[...]).astype(BF16)
+        y_copy(0, m, half).start()
+
+    def attn_finish(m):
+        for half in (0, 1):
+            y_copy(0, m, half).wait()
+            for i, k in enumerate(HALVES[half]):
+                here, there = pl.ds(k * R, R), pl.ds((half * 2 + i) * R, R)
+                total = (y_send[0, m, there, :].astype(F32) + y_recv[0, m, there, :].astype(F32)).astype(BF16)
+                h_buf[m, here, :] = (h_buf[m, here, :].astype(F32) + total.astype(F32)).astype(BF16)
+
+    def mlp_start(m):
+        y_send[1, m] = acc_buf[m].astype(BF16)
+        for half in (0, 1):
+            y_copy(1, m, half).start()
+
+    def mlp_finish(m):
+        for half in (0, 1):
+            y_copy(1, m, half).wait()
+            rows = pl.ds(half * 2 * R, 2 * R)
+            total = (y_send[1, m, rows, :].astype(F32) + y_recv[1, m, rows, :].astype(F32)).astype(BF16)
+            h_buf[m, rows, :] = (h_buf[m, rows, :].astype(F32) + total.astype(F32)).astype(BF16)
 
     def act_copies(t):
         return gather_copies(act_all, t, act_ss, act_rs)
@@ -212,59 +242,73 @@
         return pltpu.make_async_copy(h_buf.at[m, pl.ds(k * R, R)], hid_out.at[pl.ds(row, R)], o_sem.at[m, k])
 
     def mid_ready(m):
-        y_finish(0, m)
+        attn_finish(m)
         stats_start(0, m)
 
     def layer_done(m):
-        y_finish(1, m)
+        mlp_finish(m)
         if tail:
             stats_start(1, m)
         for k in range(4):
             out_copy(m, k).start()
 
-    def mlp_iter(t):
-        @pl.when((t >= O2) & (t < n_mlp + O2))
-        def _():
-            stage2(t - O2)
-
-        @pl.when((t >= O3) & (t < n_mlp + O3))
-        def _():
-            s = t - O3
-            full = stage3(s)
-            gate, up = full[:, :CW].astype(F32), full[:, CW:].astype(F32)
-            act_all[s, pl.ds(0, R), :] = (jax.nn.silu(gate) * up).astype(BF16)
-            to_core, to_chip, _ = act_copies(s)
-            to_chip().start()
-            to_core().start()
-
-        @pl.when((t >= O4) & (t < n_mlp + O4))
-        def _():
+    def split(t):
+        return (0, t) if NM == 1 else (lax.div(t, n_ffn), lax.rem(t, n_ffn))
+
+    def mlp_iter(t, steady):
+        def stage(first, action):
+            if steady:
+                action()
+            else:
+                pl.when((t >= first) & (t < n_mlp + first))(action)
+
+        def relay_on():
             _, to_chip, relay = act_copies(t - O4)
             to_chip().wait_recv()
             relay().start()
 
-        @pl.when(t < n_mlp)
-        def _():
-            m, j = (0, t) if NM == 1 else (lax.div(t, n_ffn), lax.rem(t, n_ffn))
-
-            @pl.when(t < n_ffn)
-            def _():
-                for cp in wgu_copy(t):
-                    cp.wait()
-            stage1(t, m, wgu_buf[j])
-
-        @pl.when((t >= O5) & (t < n_mlp + O5))
-        def _():
-            s = t - O5
-            m, j = (0, s) if NM == 1 else (lax.div(s, n_ffn), lax.rem(s, n_ffn))
-            to_core, _, relay = act_copies(s)
+        def act_ready():
+            to_core, _, relay = act_copies(t - O5)
             to_core().wait_recv()
             relay().wait_recv()
 
-            @pl.when(s == 0)
-            def _():
-                wd_copy.wait()
+        @pl.when(t < n_ffn)
+        def _():
+            for cp in wgu_copy(t):
+                cp.wait()
+        stage(O4, relay_on)
+        stage(O2, lambda: stage2_wait(t - O2))
+        stage(O3, lambda: x_copy(t - O3).wait_recv())
+        stage(O5, act_ready)
+        stage(0, lambda: after_ring(t, lambda: d_copy(t - ring).wait_send()))
+
+        def activate():
+            s = t - O3
+            full = stage3_sum(s)
+            gate, up = full[:, :CW].astype(F32), full[:, CW:].astype(F32)
+            act_all[s, pl.ds(0, R), :] = (jax.nn.silu(gate) * up).astype(BF16)
+
+        def product():
+            m, j = split(t)
+            stage1_math(t, m, wgu_buf[j])
+
+        def down():
+            s = t - O5
+            m, j = split(s)
             acc_buf[m] += dot(act_all[s], wd_buf[pl.ds(pl.multiple_of(j * CW, CW), CW), :])
+
+        def send_act():
+            to_core, to_chip, _ = act_copies(t - O3)
+            to_chip().start()
+            to_core().start()
+
+        stage(O2, lambda: stage2_math(t - O2))
+        stage(O3, activate)
+        stage(0, product)
+        stage(O5, down)
+        stage(O2, lambda: x_copy(t - O2).start())
+        stage(O3, send_act)
+        stage(0, lambda: d_copy(t).start())
 
     pl.semaphore_wait(barrier, 4)
 
@@ -276,36 +320,38 @@
             to_core().start()
             acc_buf[m] = jnp.zeros(acc_buf.shape[1:], F32)
         for m in range(NM):
-            _, to_chip, relay = attn_copies(m)
-            to_chip().wait_recv()
-            relay().start()
-        for m in range(NM):
             for k in range(4):
                 hid_copy(m, k).wait()
         wo_copy.wait()
         for m in range(NM):
-            to_core, _, relay = attn_copies(m)
-            to_core().wait_recv()
+            attn_copies(m)[0]().wait_recv()
+            attn_half(m, 0)
+        for m in range(NM):
+            _, to_chip, relay = attn_copies(m)
+            to_chip().wait_recv()
+            relay().start()
             relay().wait_recv()
-            y_start(0, m, dot(attn_all[m], wo_buf[...]))
-        y_finish(0, 0)
-        stats_start(0, 0)
+            attn_half(m, 1)
+        mid_ready(0)
         norm(0, 0, g_mlp[pl.ds(layer, 1), :])
         events = {}
         if NM == 2:
             first_done = n_ffn - 1 + O5
             events = {E1: lambda: mid_ready(1), E2: lambda: norm(0, 1, g_mlp[pl.ds(layer, 1), :]),
-                      first_done: lambda: y_start(1, 0, acc_buf[0]), first_done + E3: lambda: layer_done(0)}
+                      first_done: lambda: mlp_start(0), first_done + E3: lambda: layer_done(0)}
             if tail:
                 events[first_done + E4] = lambda: norm(1, 0, g_attn[pl.ds(tail_layer, 1), :])
 
-        def body(t, c):
-            mlp_iter(t)
+        def body(steady, t, c):
+            mlp_iter(t, steady)
             for at, event in events.items():
                 pl.when(t == at)(event)
             return c
-        lax.fori_loop(0, n_mlp + O5, body, 0)
-        y_start(1, NM - 1, acc_buf[NM - 1])
+        lax.fori_loop(0, O5, functools.partial(body, False), 0)
+        wd_copy.wait()
+        lax.fori_loop(O5, n_mlp, functools.partial(body, True), 0)
+        lax.fori_loop(n_mlp, n_mlp + O5, functools.partial(body, False), 0)
+        mlp_start(NM - 1)
         if not (tail and NM == 2):
             layer_done(NM - 1)
     else:
@@ -393,7 +439,7 @@
             pltpu.VMEM((NM, M, attn.shape[1]), BF16), pltpu.VMEM(wo.shape[1:], BF16), pltpu.VMEM((n_ffn, feat, IW), BF16),
             pltpu.VMEM(wd.shape[1:], BF16), pltpu.VMEM((NM, M, feat), F32), pltpu.VMEM((n_ffn * NM, M, CW), BF16),
             pltpu.VMEM((2, NM, M, feat), BF16), pltpu.VMEM((2, NM, M, feat), BF16),
-            dma((3, NM)), dma((3, NM)), dma((2, NM)), dma((2, NM)), dma((3, n_ffn * NM)), dma((3, n_ffn * NM)),
+            dma((3, NM)), dma((3, NM)), dma((2, NM, 2)), dma((2, NM, 2)), dma((3, n_ffn * NM)), dma((3, n_ffn * NM)),
             dma, dma((2, n_ffn)), dma, dma((NM, 4)), dma((NM,))]
     if tail:
         scratch += [pltpu.VMEM((6, feat, IW), BF16), dma((6,)), dma((n_pref, 2))]

time: 230 us -> 221 us (0.961)
  Pallas kernels: 218 us -> 210 us
    pallas_call x3, Pallas kernels: 189 us -> 180 us  [chain_call(): pl.pallas_call(functools.partial(chain_kernel, head, tail, layer, n_pref,...]
where the time goes in v3:
time: 221 us
  Pallas kernels  210 us (95%)
  local copies, waits for them, and re-layouts  9.21 us (4%)
    pallas_call x3, Pallas kernels, chain_call(): pl.pallas_call(functools.partial(chain_kernel, head, tail, layer, n_pref,...  180 us
    pallas_call x2, Pallas kernels, attn_call(): pl.pallas_call(functools.partial(attn_kernel, layer, n_pref), out_shape=[...  29.7 us
    unnamed x15, local copies, waits for them, and re-layouts  8.39 us

profile of v3, /device:TPU:0, one launch (start us, length us, event | category | flops | bytes accessed | tf_op | source)
XLA Modules:
  0.0 220.9 jit_solution(11791817286382458557)
XLA Ops:
  0.6 0.1 pad.5.clone
  0.7 0.8 fusion.1
  1.5 0.7 fusion.2
  2.2 0.2 multiply_cosine_fusion
  2.4 0.1 maximum_maximum_fusion.tabs_hbm
  2.6 0.0 copy-start
  2.6 1.3 copy-done
  3.9 0.0 copy-start.1
  3.9 1.3 copy-done.1
  5.2 0.0 copy-start.2
  5.2 1.0 copy-done.2
  6.2 0.0 copy-start.6
  6.2 0.7 copy-done.6
  6.8 19.1 %chain_01.1 = (bf16[6,64,512]{2,1,0:T(8,128)(2,1)S(1)}, bf16[8,2,8,1024,128]{4,3,2,1,0:T(8,128)(2,1)S(1)}) custom-call(bf16[256,640]{1,0:T(8,128)(2,1)S(1)} %copy-done.2, bf16[2,640]{1,0:T(2,128)(2,1)S(1)} %copy-done.6, bf16[2,640,2048]{2,1,0:T(8,128)(2,1)} %refs_8_.1, bf16[2,640,512]{2,1,0:T(8,128)(2,1)S(1)} %copy-done, bf16[2,640,512]{2,1,0:T(8,128)(2,1)S(1)} %copy-done.1, ...), custom_call_target="tpu_custom_call" | custom-call | tf_op jit(solution)/shard_map/chain_01/pallas_call | solution.py:446
  26.0 14.3 %attn_0.1 = (bf16[2,64,1024,128]{3,2,1,0:T(8,128)(2,1)}, bf16[2,64,1024,128]{3,2,1,0:T(8,128)(2,1)}, bf16[64,2048]{1,0:T(8,128)(2,1)S(1)}, bf16[8,2,8,1024,128]{4,3,2,1,0:T(8,128)(2,1)S(1)}) custom-call(s32[64]{0:T(128)S(1)} %get-tuple-element.18.pos_ref, bf16[6,64,512]{2,1,0:T(8,128)(2,1)S(1)} %get-tuple-element.19.qkv_hbm, ...), custom_call_target="tpu_custom_call", output_to_operand_aliasing={{3}: (5, {})} | custom-call | tf_op jit(solution)/shard_map/attn_0/pallas_call | solution.py:570
  40.3 0.0 copy-start.5
  40.3 0.7 copy-done.5
  41.0 89.5 %chain_11.1 = (bf16[256,640]{1,0:T(8,128)(2,1)}, bf16[6,64,512]{2,1,0:T(8,128)(2,1)}, bf16[5,2,8,1024,128]{4,3,2,1,0:T(8,128)(2,1)S(1)}) custom-call(bf16[256,640]{1,0:T(8,128)(2,1)} %refs_0_.1, bf16[64,2048]{1,0:T(8,128)(2,1)} %copy-done.5, bf16[2,640]{1,0:T(2,128)(2,1)} %refs_2_.5, bf16[2,2048,640]{2,1,0:T(8,128)(2,1)} %refs_3_.5, ...), custom_call_target="tpu_custom_call" | custom-call | tf_op jit(solution)/shard_map/chain_11/pallas_call | solution.py:446
  130.5 0.0 copy-start.3
  130.5 1.0 copy-done.3
  131.5 15.5 %attn_1.1 = (bf16[2,64,1024,128]{3,2,1,0:T(8,128)(2,1)}, bf16[2,64,1024,128]{3,2,1,0:T(8,128)(2,1)}, bf16[64,2048]{1,0:T(8,128)(2,1)S(1)}, bf16[5,2,8,1024,128]{4,3,2,1,0:T(8,128)(2,1)S(1)}) custom-call(s32[64]{0:T(128)S(1)} %get-tuple-element.18.pos_ref, ...), custom_call_target="tpu_custom_call", output_to_operand_aliasing={{3}: (5, {}), {0}: (6, {}), {1}: (7, {})} | custom-call | tf_op jit(solution)/shard_map/attn_1/pallas_call | solution.py:570
  146.9 0.0 copy-start.4
  147.0 0.7 copy-done.4
  147.6 71.5 %chain_10.1 = bf16[256,640]{1,0:T(8,128)(2,1)} custom-call(bf16[256,640]{1,0:T(8,128)(2,1)} %get-tuple-element.23.refs_0_, bf16[64,2048]{1,0:T(8,128)(2,1)} %copy-done.4, bf16[2,640]{1,0:T(2,128)(2,1)} %refs_2_.5, bf16[2,2048,640]{2,1,0:T(8,128)(2,1)} %refs_3_.5, bf16[2,640,4864]{2,1,0:T(8,128)(2,1)} %refs_4_.5, bf16[2,640,4864]{2,1,0:T(8,128)(2,1)} %refs_5_.3, ...), custom_call_target="tpu_custom_call" | custom-call | tf_op jit(solution)/shard_map/chain_10/pallas_call | solution.py:446
  219.2 1.7 copy.27
  (3 shorter events, 0.0 us)
Async XLA Ops:
  2.6 1.3 copy-start
  3.9 1.3 copy-start.1
  5.2 1.0 copy-start.2
  6.2 0.7 copy-start.6
  40.3 0.7 copy-start.5
  130.5 1.0 copy-start.3
  146.9 0.7 copy-start.4

commit v4 on v3

--- a/solution.py
+++ b/solution.py
@@ -18,16 +18,22 @@
 IW = 2 * CW
 O2, O3, O4, O5 = 3, 8, 13, 16
 E1, E2, E3, E4 = 2, 8, 6, 10
+HEAD_GROUPS = 2
 RING = 8
 SB = 8
+AHEAD = 2
 NBUF = 3
 MASK = (0, 2, 1, 3)
 POS = (0, 2, 1, 3)
 HALVES = ((0, 2), (1, 3))
 
 
+def in_hbm(x):
+    return pltpu.with_memory_space_constraint(x, pltpu.HBM)
+
+
 def groups(head):
-    return 2 if head else 1
+    return HEAD_GROUPS if head else 1
 
 
 def dot(a, b):
@@ -39,17 +45,18 @@
     it = iter(refs)
     hid_in = next(it)
     if head:
-        attn_in, g_mlp = next(it), next(it)
+        attn_in, g_mlp_in = next(it), next(it)
         wo_in, wg_in, wu_in, wd_in = (next(it).at[layer] for _ in range(4))
     if tail:
         tail_layer = layer + 1 if head else layer
-        g_attn = next(it)
+        g_attn_in = next(it)
         wq_in, wk_in, wv_in, k_in, v_in = (next(it).at[tail_layer] for _ in range(5))
     if head:
         hid_out = next(it)
     if tail:
         qkv_out, pref_out = next(it), next(it)
     h_buf, n_buf, stat_buf, keep_buf, own_buf, dsend, drecv, xsend, xrecv = (next(it) for _ in range(9))
+    gain_buf, gain_sem = next(it), next(it)
     h_sem, st_ss, st_rs, d_ss, d_rs, x_ss, x_rs = (next(it) for _ in range(7))
     if head:
         attn_all, wo_buf, wgu_buf, wd_buf, acc_buf, act_all, y_send, y_recv = (next(it) for _ in range(8))
@@ -99,6 +106,13 @@
     for m in range(NM):
         for k in range(4):
             hid_copy(m, k).start()
+    gain_copies = []
+    if head:
+        gain_copies.append(pltpu.make_async_copy(g_mlp_in, gain_buf.at[0], gain_sem.at[0]))
+    if tail:
+        gain_copies.append(pltpu.make_async_copy(g_attn_in, gain_buf.at[1], gain_sem.at[1]))
+    for cp in gain_copies:
+        cp.start()
 
     def wgu_copy(j):
         off = pl.multiple_of(j * CW, CW)
@@ -111,23 +125,20 @@
     if tail:
         wqkv_copies = [pltpu.make_async_copy(wq_in.at[:, pl.ds(j * IW, IW)], wqkv_buf.at[j], wqkv_sem.at[j]) for j in range(4)]
         wqkv_copies += [pltpu.make_async_copy(w, wqkv_buf.at[j], wqkv_sem.at[j]) for j, w in ((4, wk_in), (5, wv_in))]
+    def start_wgu(j, c):
+        for cp in wgu_copy(j):
+            cp.start()
+        return c
     if head:
         wo_copy.start()
-
-        def start_wgu(j, c):
-            for cp in wgu_copy(j):
-                cp.start()
-            return c
-        lax.fori_loop(0, n_ffn, start_wgu, 0)
-        wd_copy.start()
-    if tail:
+    else:
         for cp in wqkv_copies:
             cp.start()
 
     def pref_copy(blk, c):
         seqs = pl.ds(blk * SB, SB)
         return pltpu.make_async_copy((k_in, v_in)[c].at[seqs], pref_out.at[blk, c], pref_sem.at[blk, c])
-    if tail:
+    def pref_start():
         for blk in range(n_pref):
             for c in (0, 1):
                 pref_copy(blk, c).start()
@@ -311,6 +322,8 @@
         stage(0, lambda: d_copy(t).start())
 
     pl.semaphore_wait(barrier, 4)
+    for cp in gain_copies:
+        cp.wait()
 
     if head:
         for m in range(NM):
@@ -323,6 +336,11 @@
             for k in range(4):
                 hid_copy(m, k).wait()
         wo_copy.wait()
+        lax.fori_loop(0, n_ffn, start_wgu, 0)
+        wd_copy.start()
+        if tail:
+            for cp in wqkv_copies:
+                cp.start()
         for m in range(NM):
             attn_copies(m)[0]().wait_recv()
             attn_half(m, 0)
@@ -333,26 +351,37 @@
             relay().wait_recv()
             attn_half(m, 1)
         mid_ready(0)
-        norm(0, 0, g_mlp[pl.ds(layer, 1), :])
+        norm(0, 0, gain_buf[0, pl.ds(layer, 1), :])
+        if tail:
+            pref_start()
         events = {}
-        if NM == 2:
-            first_done = n_ffn - 1 + O5
-            events = {E1: lambda: mid_ready(1), E2: lambda: norm(0, 1, g_mlp[pl.ds(layer, 1), :]),
-                      first_done: lambda: mlp_start(0), first_done + E3: lambda: layer_done(0)}
+
+        def at(t, action, *operands):
+            events.setdefault(t, []).append(functools.partial(action, *operands))
+        for m in range(1, NM):
+            at((m - 1) * n_ffn + E1, mid_ready, m)
+            at((m - 1) * n_ffn + E2, lambda m: norm(0, m, gain_buf[0, pl.ds(layer, 1), :]), m)
+        for m in range(NM - 1):
+            done = (m + 1) * n_ffn - 1 + O5
+            at(done, mlp_start, m)
+            at(min(done + E3, n_mlp + O5 - 2), layer_done, m)
             if tail:
-                events[first_done + E4] = lambda: norm(1, 0, g_attn[pl.ds(tail_layer, 1), :])
+                at(min(done + E4, n_mlp + O5 - 1), lambda m: norm(1, m, gain_buf[1, pl.ds(tail_layer, 1), :]), m)
 
         def body(steady, t, c):
             mlp_iter(t, steady)
-            for at, event in events.items():
-                pl.when(t == at)(event)
+            for when, actions in events.items():
+                @pl.when(t == when)
+                def _(actions=actions):
+                    for action in actions:
+                        action()
             return c
         lax.fori_loop(0, O5, functools.partial(body, False), 0)
         wd_copy.wait()
         lax.fori_loop(O5, n_mlp, functools.partial(body, True), 0)
         lax.fori_loop(n_mlp, n_mlp + O5, functools.partial(body, False), 0)
         mlp_start(NM - 1)
-        if not (tail and NM == 2):
+        if not tail:
             layer_done(NM - 1)
     else:
         for m in range(NM):
@@ -363,16 +392,18 @@
     if tail:
         for cp in wqkv_copies:
             cp.wait()
+        if not head:
+            pref_start()
         n_all = n_qkv * NM
-        if not (head and NM == 2):
+        if not head:
             for m in range(NM):
-                norm(1, m, g_attn[pl.ds(tail_layer, 1), :])
+                norm(1, m, gain_buf[1, pl.ds(tail_layer, 1), :])
         for t in range(n_all + 3):
             if 1 <= t < n_all + 1:
                 stage2(n_mlp + t - 1)
-            if head and NM == 2 and t == n_qkv:
-                layer_done(1)
-                norm(1, 1, g_attn[pl.ds(tail_layer, 1), :])
+            if head and t == n_qkv * (NM - 1):
+                layer_done(NM - 1)
+                norm(1, NM - 1, gain_buf[1, pl.ds(tail_layer, 1), :])
             if t < n_all:
                 stage1(n_mlp + t, t // n_qkv, wqkv_buf[t % n_qkv])
             if t >= 3:
@@ -409,19 +440,19 @@
     R = M // 4
     vmem = pl.BlockSpec(memory_space=pltpu.VMEM)
     hbm = pl.BlockSpec(memory_space=pltpu.HBM)
-    args, in_specs = [hidden], [hbm]
+    args, in_specs = [in_hbm(hidden)], [hbm]
     out_shape, out_specs = [], []
     n_items = 0
     if head:
-        args += [attn, g_mlp, wo, wg, wu, wd]
-        in_specs += [hbm, vmem, hbm, hbm, hbm, hbm]
+        args += [attn, in_hbm(g_mlp), in_hbm(wo), in_hbm(wg), in_hbm(wu), in_hbm(wd)]
+        in_specs += [hbm] * 6
         out_shape.append(jax.ShapeDtypeStruct(hidden.shape, hidden.dtype))
         out_specs.append(hbm)
         n_ffn = wg.shape[2] // CW
         n_items += n_ffn * NM
     if tail:
-        args += [g_attn, wq, wk, wv, k_rows, v_rows]
-        in_specs += [vmem] + [hbm] * 5
+        args += [in_hbm(g_attn), in_hbm(wq), in_hbm(wk), in_hbm(wv), in_hbm(k_rows), in_hbm(v_rows)]
+        in_specs += [hbm] * 6
         out_shape.append(jax.ShapeDtypeStruct((6, batch // 4, IW), BF16))
         out_specs.append(vmem)
         out_shape.append(pltpu.VMEM((n_pref, 2, SB) + k_rows.shape[2:], BF16))
@@ -433,6 +464,7 @@
         pltpu.VMEM((O2 + 1, 2 * R, IW), F32), pltpu.VMEM((O3 - O2 + 1, R, IW), F32),
         pltpu.VMEM((RING, 2 * R, IW), BF16), pltpu.VMEM((n_items, 2 * R, IW), BF16),
         pltpu.VMEM((RING, R, IW), BF16), pltpu.VMEM((n_items, R, IW), BF16),
+        pltpu.VMEM((2,) + (g_mlp if head else g_attn).shape, BF16), dma((2,)),
         dma((NM, 4)), dma((2, NM, 3)), dma((2, NM, 3)), dma((n_items,)), dma((n_items,)), dma((n_items,)), dma((n_items,))]
     if head:
         scratch += [
@@ -451,9 +483,10 @@
     )(*args)
 
 
-def attn_kernel(layer, n_pref, pos_ref, qkv_hbm, tabs_hbm, k_hbm, v_hbm, *refs):
-    k_out, v_out, o_ref, pref, kv_slots, q_buf, kv_buf, o_buf, s_buf, p_buf, qkv_ref, tabs_ref, in_sem, out_sem, small_sem = refs[-15:]
-    small = (pltpu.make_async_copy(qkv_hbm, qkv_ref, small_sem.at[0]), pltpu.make_async_copy(tabs_hbm, tabs_ref, small_sem.at[1]))
+def attn_kernel(layer, n_pref, pos_hbm, qkv_hbm, tabs_hbm, k_hbm, v_hbm, *refs):
+    k_out, v_out, o_ref, pref, kv_slots, q_buf, kv_buf, o_buf, s_buf, p_buf, qkv_ref, tabs_ref, pos_ref, in_sem, out_sem, small_sem = refs[-16:]
+    small = (pltpu.make_async_copy(qkv_hbm, qkv_ref, small_sem.at[0]), pltpu.make_async_copy(tabs_hbm, tabs_ref, small_sem.at[1]),
+             pltpu.make_async_copy(pos_hbm, pos_ref, small_sem.at[2]))
     for cp in small:
         cp.start()
     local = o_ref.shape[0]
@@ -491,8 +524,6 @@
     def norm_rope(vals, gain):
         normed = vals * lax.rsqrt(jnp.mean(vals * vals, axis=-1, keepdims=True) + NORM_EPS) * gain
         return (normed * cos_tab + pltpu.roll(normed, HEAD_DIM // 2, 1) * sin_tab).astype(BF16).astype(F32)
-    for h in range(n_q):
-        q_buf[pl.ds(h * local, local), :] = norm_rope(head_of(h), gains[0])
     for h in range(n_kv):
         kv_buf[0, pl.ds(h * local, local), :] = norm_rope(head_of(n_q + h), gains[1])
         kv_buf[1, pl.ds(h * local, local), :] = head_of(n_q + n_kv + h)
@@ -502,10 +533,8 @@
     head_hit = lax.rem(lane_ids, n_kv) == lax.div(lax.broadcasted_iota(jnp.int32, (n_q, n_rows), 0), group)
     lane_of = jnp.where(head_hit, lane_ids, n_rows)
 
-    def block_step(blk, early):
+    def patch(blk, early):
         ref = held(blk, early)
-        if not early:
-            run(blk, False, False, True)
         for i in range(SB):
             b = blk * SB + i
             row = pos_ref[b] * n_kv
@@ -516,10 +545,32 @@
                 new = jnp.concatenate([new] * (16 // n_kv), axis=0)
                 old = ref[c, i, pl.ds(base, 16), :]
                 ref[c, i, pl.ds(base, 16), :] = jnp.where(hit, new, old.astype(F32)).astype(BF16)
+
+    for blk in range(min(AHEAD, n_pref)):
+        patch(blk, True)
+    for h in range(n_q):
+        q_buf[pl.ds(h * local, local), :] = norm_rope(head_of(h), gains[0])
+    for blk in range(min(AHEAD, n_pref)):
+        run(blk, True, True, False)
+
+    def block_step(blk, early):
+        ref = held(blk, early)
+        if early:
+            @pl.when(blk + AHEAD < n_pref)
+            def _():
+                patch(blk + AHEAD, True)
+        else:
+            run(blk, False, False, True)
+            patch(blk, False)
         for i in range(SB):
             q = q_buf[pl.ds(blk * SB + i, n_q, stride=local), :].astype(BF16)
             s_buf[i] = lax.dot_general(q, ref[0, i], (((1,), (1,)), ((), ())), preferred_element_type=F32)
-        run(blk, early, True, False)
+        if early:
+            @pl.when(blk + AHEAD < n_pref)
+            def _():
+                run(blk + AHEAD, True, True, False)
+        else:
+            run(blk, False, True, False)
         for i in range(SB):
             row = pos_ref[blk * SB + i] * n_kv
             scores = jnp.where(lane_of < row + n_kv, s_buf[i] * (HEAD_DIM ** -0.5), -1e30)
@@ -556,11 +607,10 @@
     layers, local, n_rows, _ = k_cache.shape
     n_kv = 4
     n_q = 16
-    smem = pl.BlockSpec(memory_space=pltpu.SMEM)
     vmem = pl.BlockSpec(memory_space=pltpu.VMEM)
     hbm = pl.BlockSpec(memory_space=pltpu.HBM)
-    args = [pos, qkv, tabs, k_cache, v_cache, pref]
-    in_specs = [smem, hbm, hbm, hbm, hbm, vmem]
+    args = [in_hbm(pos), qkv if layer == 0 else in_hbm(qkv), in_hbm(tabs), in_hbm(k_cache), in_hbm(v_cache), pltpu.with_memory_space_constraint(pref, pltpu.VMEM)]
+    in_specs = [hbm, hbm, hbm, hbm, hbm, vmem]
     aliases = {5: 3}
     n_pref, n_blocks = pref.shape[0], local // SB
     if prev is not None:
@@ -575,10 +625,10 @@
         scratch_shapes=[pltpu.VMEM((min(NBUF, max(n_blocks - n_pref, 1)) if n_pref < n_blocks else 1, 2, SB if n_pref < n_blocks else 1, n_rows, HEAD_DIM), BF16),
                         pltpu.VMEM((n_q * local, HEAD_DIM), F32), pltpu.VMEM((2, n_kv * local, HEAD_DIM), F32), pltpu.VMEM((n_q * local, HEAD_DIM), F32),
                         pltpu.VMEM((SB, n_q, n_rows), F32), pltpu.VMEM((SB, n_q, n_rows), BF16),
-                        pltpu.VMEM(qkv.shape, BF16), pltpu.VMEM(tabs.shape, F32),
-                        pltpu.SemaphoreType.DMA((n_blocks, 2)), pltpu.SemaphoreType.DMA((n_blocks, 2)), pltpu.SemaphoreType.DMA((2,))],
+                        pltpu.VMEM(qkv.shape, BF16), pltpu.VMEM(tabs.shape, F32), pltpu.SMEM(pos.shape, jnp.int32),
+                        pltpu.SemaphoreType.DMA((n_blocks, 2)), pltpu.SemaphoreType.DMA((n_blocks, 2)), pltpu.SemaphoreType.DMA((3,))],
         input_output_aliases=aliases, name=f'attn_{layer}',
-        compiler_params=pltpu.CompilerParams(vmem_limit_bytes=(20 if n_pref == n_blocks else 22) * 1024 * 1024),
+        compiler_params=pltpu.CompilerParams(vmem_limit_bytes=(20 if layer == 0 else 22) * 1024 * 1024),
     )(*args)
 
 
@@ -609,7 +659,7 @@
         k_new, v_new, attn, _ = attn_call(0, my_pos, qkv, *attn_tabs, pref, None)
         hidden, qkv, pref = chain_call(True, True, 0, 1, 5, 40, model_dim, hidden, attn, g_mlp, w_o, w_gate, w_up, w_down, g_attn, w_q, w_k, w_v, **caches)
         k_new, v_new, attn, _ = attn_call(1, my_pos, qkv, *attn_tabs, pref, (k_new, v_new))
-        (hidden,) = chain_call(True, False, 1, 2, 0, 60, model_dim, hidden, attn, g_mlp, w_o, w_gate, w_up, w_down)
+        (hidden,) = chain_call(True, False, 1, 2, 0, 46, model_dim, hidden, attn, g_mlp, w_o, w_gate, w_up, w_down)
         return hidden, k_new.reshape(k_cache.shape), v_new.reshape(v_cache.shape)
 
     return jax.shard_map(device_step, mesh=mesh, in_specs=in_specs, out_specs=out_specs, check_vma=False)

time: 221 us -> 215 us (0.973)
  local copies, waits for them, and re-layouts: 9.21 us -> 2.24 us
    unnamed x15 -> x3, local copies, waits for them, and re-layouts: 8.39 us -> 1.42 us
where the time goes in v4:
time: 215 us
  Pallas kernels  209 us (97%)
  other arithmetic  2.28 us (1%)
  local copies, waits for them, and re-layouts  2.24 us (1%)
    pallas_call x3, Pallas kernels, chain_call(): pl.pallas_call(functools.partial(chain_kernel, head, tail, layer, n_pref,...  180 us
    pallas_call x2, Pallas kernels, attn_call(): pl.pallas_call(functools.partial(attn_kernel, layer, n_pref), out_shape=[...  29.4 us

profile of v4, /device:TPU:0, one launch (start us, length us, event | category | flops | bytes accessed | tf_op | source)
XLA Modules:
  0.0 214.6 jit_solution(2982010487583084608)
XLA Ops:
  0.6 0.1 pad.5.clone
  0.7 1.3 fusion.1
  2.1 0.7 fusion.2
  2.8 0.2 multiply_cosine_fusion
  3.0 0.7 maximum_maximum_fusion.tabs_hbm
  3.7 19.2 %chain_01.1 = (bf16[6,64,512]{2,1,0:T(8,128)(2,1)S(1)}, bf16[8,2,8,1024,128]{4,3,2,1,0:T(8,128)(2,1)S(1)}) custom-call(bf16[256,640]{1,0:T(8,128)(2,1)} %refs_0_.1, bf16[2,640]{1,0:T(2,128)(2,1)} %refs_7_.1, bf16[2,640,2048]{2,1,0:T(8,128)(2,1)} %refs_8_.1, bf16[2,640,512]{2,1,0:T(8,128)(2,1)} %refs_9_.1, bf16[2,640,512]{2,1,0:T(8,128)(2,1)} %refs_10_.1, ...), custom_call_target="tpu_custom_call" | custom-call | tf_op jit(solution)/shard_map/chain_01/pallas_call | solution.py:478
  23.0 13.5 %attn_0.1 = (bf16[2,64,1024,128]{3,2,1,0:T(8,128)(2,1)}, bf16[2,64,1024,128]{3,2,1,0:T(8,128)(2,1)}, bf16[64,2048]{1,0:T(8,128)(2,1)S(1)}, bf16[8,2,8,1024,128]{4,3,2,1,0:T(8,128)(2,1)S(1)}) custom-call(s32[64]{0:T(128)} %get-tuple-element.18.pos_hbm, bf16[6,64,512]{2,1,0:T(8,128)(2,1)S(1)} %get-tuple-element.19.qkv_hbm, ...), custom_call_target="tpu_custom_call", output_to_operand_aliasing={{3}: (5, {})} | custom-call | tf_op jit(solution)/shard_map/attn_0/pallas_call | solution.py:620
  36.5 0.0 copy-start
  36.5 0.7 copy-done
  37.2 89.7 %chain_11.1 = (bf16[256,640]{1,0:T(8,128)(2,1)}, bf16[6,64,512]{2,1,0:T(8,128)(2,1)}, bf16[5,2,8,1024,128]{4,3,2,1,0:T(8,128)(2,1)S(1)}) custom-call(bf16[256,640]{1,0:T(8,128)(2,1)} %refs_0_.1, bf16[64,2048]{1,0:T(8,128)(2,1)} %copy-done, bf16[2,640]{1,0:T(2,128)(2,1)} %refs_2_.5, bf16[2,2048,640]{2,1,0:T(8,128)(2,1)} %refs_3_.5, ...), custom_call_target="tpu_custom_call" | custom-call | tf_op jit(solution)/shard_map/chain_11/pallas_call | solution.py:478
  126.9 15.9 %attn_1.1 = (bf16[2,64,1024,128]{3,2,1,0:T(8,128)(2,1)}, bf16[2,64,1024,128]{3,2,1,0:T(8,128)(2,1)}, bf16[64,2048]{1,0:T(8,128)(2,1)S(1)}, bf16[5,2,8,1024,128]{4,3,2,1,0:T(8,128)(2,1)S(1)}) custom-call(s32[64]{0:T(128)} %get-tuple-element.18.pos_hbm, ...), custom_call_target="tpu_custom_call", output_to_operand_aliasing={{3}: (5, {}), {0}: (6, {}), {1}: (7, {})} | custom-call | tf_op jit(solution)/shard_map/attn_1/pallas_call | solution.py:620
  142.9 70.9 %chain_10.1 = bf16[256,640]{1,0:T(8,128)(2,1)S(1)} custom-call(bf16[256,640]{1,0:T(8,128)(2,1)} %get-tuple-element.23.refs_0_, bf16[64,2048]{1,0:T(8,128)(2,1)S(1)} %get-tuple-element.28.refs_1_, bf16[2,640]{1,0:T(2,128)(2,1)} %refs_2_.5, bf16[2,2048,640]{2,1,0:T(8,128)(2,1)} %refs_3_.5, bf16[2,640,4864]{2,1,0:T(8,128)(2,1)} %refs_4_.5, ...), custom_call_target="tpu_custom_call" | custom-call | tf_op jit(solution)/shard_map/chain_10/pallas_call | solution.py:478
  213.8 0.7 copy.27
  (3 shorter events, 0.0 us)
Async XLA Ops:
  36.5 0.7 copy-start

commit v5 on v4

--- a/solution.py
+++ b/solution.py
@@ -18,6 +18,7 @@
 IW = 2 * CW
 O2, O3, O4, O5 = 3, 8, 13, 16
 E1, E2, E3, E4 = 2, 8, 6, 10
+QKV_LAG = 2
 HEAD_GROUPS = 2
 RING = 8
 SB = 8
@@ -394,21 +395,29 @@
             cp.wait()
         if not head:
             pref_start()
-        n_all = n_qkv * NM
-        if not head:
-            for m in range(NM):
-                norm(1, m, gain_buf[1, pl.ds(tail_layer, 1), :])
-        for t in range(n_all + 3):
-            if 1 <= t < n_all + 1:
-                stage2(n_mlp + t - 1)
-            if head and t == n_qkv * (NM - 1):
-                layer_done(NM - 1)
-                norm(1, NM - 1, gain_buf[1, pl.ds(tail_layer, 1), :])
-            if t < n_all:
-                stage1(n_mlp + t, t // n_qkv, wqkv_buf[t % n_qkv])
-            if t >= 3:
-                m, j = divmod(t - 3, n_qkv)
-                qkv_out[j, pl.ds(m * R, R), :] = stage3(n_mlp + t - 3)
+
+        def qkv_send(m):
+            first = n_mlp + m * n_qkv
+            for t in range(n_qkv + QKV_LAG):
+                if t < n_qkv:
+                    stage1(first + t, m, wqkv_buf[t])
+                if t >= QKV_LAG:
+                    stage2(first + t - QKV_LAG)
+
+        def qkv_take(m):
+            for j in range(n_qkv):
+                qkv_out[j, pl.ds(m * R, R), :] = stage3(n_mlp + m * n_qkv + j)
+
+        last = NM - 1
+        for m in range(last):
+            qkv_send(m)
+        if head:
+            layer_done(last)
+        for m in range(last):
+            qkv_take(m)
+        norm(1, last, gain_buf[1, pl.ds(tail_layer, 1), :])
+        qkv_send(last)
+        qkv_take(last)
 
     if tail:
         for blk in range(n_pref):
@@ -461,7 +470,7 @@
     dma = pltpu.SemaphoreType.DMA
     scratch = [
         pltpu.VMEM((NM, M, feat), BF16), pltpu.VMEM((NM, M, feat), BF16), pltpu.VMEM((2, NM, 4, 8, 128), F32),
-        pltpu.VMEM((O2 + 1, 2 * R, IW), F32), pltpu.VMEM((O3 - O2 + 1, R, IW), F32),
+        pltpu.VMEM((max(O2, QKV_LAG) + 1, 2 * R, IW), F32), pltpu.VMEM((max(O3 - O2 + 1, 6), R, IW), F32),
         pltpu.VMEM((RING, 2 * R, IW), BF16), pltpu.VMEM((n_items, 2 * R, IW), BF16),
         pltpu.VMEM((RING, R, IW), BF16), pltpu.VMEM((n_items, R, IW), BF16),
         pltpu.VMEM((2,) + (g_mlp if head else g_attn).shape, BF16), dma((2,)),
@@ -553,24 +562,17 @@
     for blk in range(min(AHEAD, n_pref)):
         run(blk, True, True, False)
 
-    def block_step(blk, early):
+    def block_step(blk, early, nxt, nxt_early):
         ref = held(blk, early)
-        if early:
-            @pl.when(blk + AHEAD < n_pref)
-            def _():
-                patch(blk + AHEAD, True)
-        else:
-            run(blk, False, False, True)
-            patch(blk, False)
+        if nxt is not None:
+            if not nxt_early:
+                run(nxt, False, False, True)
+            patch(nxt, nxt_early)
         for i in range(SB):
             q = q_buf[pl.ds(blk * SB + i, n_q, stride=local), :].astype(BF16)
             s_buf[i] = lax.dot_general(q, ref[0, i], (((1,), (1,)), ((), ())), preferred_element_type=F32)
-        if early:
-            @pl.when(blk + AHEAD < n_pref)
-            def _():
-                run(blk + AHEAD, True, True, False)
-        else:
-            run(blk, False, True, False)
+        if nxt is not None:
+            run(nxt, nxt_early, True, False)
         for i in range(SB):
             row = pos_ref[blk * SB + i] * n_kv
             scores = jnp.where(lane_of < row + n_kv, s_buf[i] * (HEAD_DIM ** -0.5), -1e30)
@@ -580,20 +582,12 @@
             o_buf[pl.ds(blk * SB + i, n_q, stride=local), :] = dot(p_buf[i], ref[1, i])
 
     def early_step(blk, carry):
-        block_step(blk, True)
+        block_step(blk, True, blk + AHEAD, True)
         return carry
-
-    def late_step(blk, carry):
-        block_step(blk, False)
-
-        @pl.when((blk > n_pref) & (blk - 1 + NBUF < n_blocks))
-        def _():
-            run(blk - 1, False, True, True)
-            run(blk - 1 + NBUF, False, False, False)
-        return carry
-    lax.fori_loop(0, n_pref, early_step, 0)
-    if n_pref < n_blocks:
-        lax.fori_loop(n_pref, n_blocks, late_step, 0)
+    lax.fori_loop(0, n_pref - AHEAD, early_step, 0)
+    for blk in range(n_pref - AHEAD, n_blocks):
+        nxt = blk + AHEAD if blk + AHEAD < n_blocks else None
+        block_step(blk, blk < n_pref, nxt, False)
 
     for h in range(n_q):
         o_ref[:, pl.ds(h * HEAD_DIM, HEAD_DIM)] = o_buf[pl.ds(h * local, local), :].astype(BF16)

time: 215 us -> 208 us (0.967)
  Pallas kernels: 209 us -> 203 us
    pallas_call x3, Pallas kernels: 180 us -> 174 us  [chain_call(): pl.pallas_call(functools.partial(chain_kernel, head, tail, layer, n_pref,...]
where the time goes in v5:
time: 208 us
  Pallas kernels  203 us (98%)
  other arithmetic  2.28 us (1%)
  local copies, waits for them, and re-layouts  2.24 us (1%)
    pallas_call x3, Pallas kernels, chain_call(): pl.pallas_call(functools.partial(chain_kernel, head, tail, layer, n_pref,...  174 us
    pallas_call x2, Pallas kernels, attn_call(): pl.pallas_call(functools.partial(attn_kernel, layer, n_pref), out_shape=[...  28.6 us

profile of v5, /device:TPU:0, one launch (start us, length us, event | category | flops | bytes accessed | tf_op | source)
XLA Modules:
  0.0 207.8 jit_solution(13429624538913032097)
XLA Ops:
  0.6 0.1 pad.5.clone
  0.7 1.3 fusion.1
  2.1 0.7 fusion.2
  2.8 0.2 multiply_cosine_fusion
  3.0 0.7 maximum_maximum_fusion.tabs_hbm
  3.7 18.9 %chain_01.1 = (bf16[6,64,512]{2,1,0:T(8,128)(2,1)S(1)}, bf16[8,2,8,1024,128]{4,3,2,1,0:T(8,128)(2,1)S(1)}) custom-call(bf16[256,640]{1,0:T(8,128)(2,1)} %refs_0_.1, bf16[2,640]{1,0:T(2,128)(2,1)} %refs_7_.1, bf16[2,640,2048]{2,1,0:T(8,128)(2,1)} %refs_8_.1, bf16[2,640,512]{2,1,0:T(8,128)(2,1)} %refs_9_.1, bf16[2,640,512]{2,1,0:T(8,128)(2,1)} %refs_10_.1, ...), custom_call_target="tpu_custom_call" | custom-call | tf_op jit(solution)/shard_map/chain_01/pallas_call | solution.py:487
  22.6 13.5 %attn_0.1 = (bf16[2,64,1024,128]{3,2,1,0:T(8,128)(2,1)}, bf16[2,64,1024,128]{3,2,1,0:T(8,128)(2,1)}, bf16[64,2048]{1,0:T(8,128)(2,1)S(1)}, bf16[8,2,8,1024,128]{4,3,2,1,0:T(8,128)(2,1)S(1)}) custom-call(s32[64]{0:T(128)} %get-tuple-element.18.pos_hbm, bf16[6,64,512]{2,1,0:T(8,128)(2,1)S(1)} %get-tuple-element.19.qkv_hbm, ...), custom_call_target="tpu_custom_call", output_to_operand_aliasing={{3}: (5, {})} | custom-call | tf_op jit(solution)/shard_map/attn_0/pallas_call | solution.py:614
  36.1 0.0 copy-start
  36.1 0.7 copy-done
  36.8 84.0 %chain_11.1 = (bf16[256,640]{1,0:T(8,128)(2,1)}, bf16[6,64,512]{2,1,0:T(8,128)(2,1)}, bf16[5,2,8,1024,128]{4,3,2,1,0:T(8,128)(2,1)S(1)}) custom-call(bf16[256,640]{1,0:T(8,128)(2,1)} %refs_0_.1, bf16[64,2048]{1,0:T(8,128)(2,1)} %copy-done, bf16[2,640]{1,0:T(2,128)(2,1)} %refs_2_.5, bf16[2,2048,640]{2,1,0:T(8,128)(2,1)} %refs_3_.5, ...), custom_call_target="tpu_custom_call" | custom-call | tf_op jit(solution)/shard_map/chain_11/pallas_call | solution.py:487
  120.8 15.1 %attn_1.1 = (bf16[2,64,1024,128]{3,2,1,0:T(8,128)(2,1)}, bf16[2,64,1024,128]{3,2,1,0:T(8,128)(2,1)}, bf16[64,2048]{1,0:T(8,128)(2,1)S(1)}, bf16[5,2,8,1024,128]{4,3,2,1,0:T(8,128)(2,1)S(1)}) custom-call(s32[64]{0:T(128)} %get-tuple-element.18.pos_hbm, ...), custom_call_target="tpu_custom_call", output_to_operand_aliasing={{3}: (5, {}), {0}: (6, {}), {1}: (7, {})} | custom-call | tf_op jit(solution)/shard_map/attn_1/pallas_call | solution.py:614
  135.9 71.2 %chain_10.1 = bf16[256,640]{1,0:T(8,128)(2,1)S(1)} custom-call(bf16[256,640]{1,0:T(8,128)(2,1)} %get-tuple-element.23.refs_0_, bf16[64,2048]{1,0:T(8,128)(2,1)S(1)} %get-tuple-element.28.refs_1_, bf16[2,640]{1,0:T(2,128)(2,1)} %refs_2_.5, bf16[2,2048,640]{2,1,0:T(8,128)(2,1)} %refs_3_.5, bf16[2,640,4864]{2,1,0:T(8,128)(2,1)} %refs_4_.5, ...), custom_call_target="tpu_custom_call" | custom-call | tf_op jit(solution)/shard_map/chain_10/pallas_call | solution.py:487
  207.1 0.7 copy.27
  (3 shorter events, 0.0 us)
Async XLA Ops:
  36.1 0.7 copy-start

commit v6 on v5

--- a/solution.py
+++ b/solution.py
@@ -2,6 +2,7 @@
 
 import jax
 import jax.numpy as jnp
+import numpy as np
 from jax import lax
 from jax.experimental import pallas as pl
 from jax.experimental.pallas import tpu as pltpu
@@ -16,8 +17,8 @@
 
 CW = 256
 IW = 2 * CW
-O2, O3, O4, O5 = 3, 8, 13, 16
-E1, E2, E3, E4 = 2, 8, 6, 10
+O2, O3, O4, O5 = 2, 8, 14, 16
+E1, E2, E3, E4 = 6, 12, 8, 14
 QKV_LAG = 2
 HEAD_GROUPS = 2
 RING = 8
@@ -492,10 +493,11 @@
     )(*args)
 
 
-def attn_kernel(layer, n_pref, pos_hbm, qkv_hbm, tabs_hbm, k_hbm, v_hbm, *refs):
-    k_out, v_out, o_ref, pref, kv_slots, q_buf, kv_buf, o_buf, s_buf, p_buf, qkv_ref, tabs_ref, pos_ref, in_sem, out_sem, small_sem = refs[-16:]
-    small = (pltpu.make_async_copy(qkv_hbm, qkv_ref, small_sem.at[0]), pltpu.make_async_copy(tabs_hbm, tabs_ref, small_sem.at[1]),
-             pltpu.make_async_copy(pos_hbm, pos_ref, small_sem.at[2]))
+def attn_kernel(layer, n_pref, pos_hbm, qkv_hbm, cos_hbm, sin_hbm, qg_hbm, kg_hbm, k_hbm, v_hbm, *refs):
+    k_out, v_out, o_ref, pref, kv_slots, q_buf, kv_buf, o_buf, s_buf, p_buf, qkv_ref, tabs_ref, pos_ref, gain_ref, in_sem, out_sem, small_sem = refs[-17:]
+    small = (pltpu.make_async_copy(qkv_hbm, qkv_ref, small_sem.at[0]), pltpu.make_async_copy(cos_hbm, tabs_ref.at[0], small_sem.at[1]), pltpu.make_async_copy(sin_hbm, tabs_ref.at[1], small_sem.at[5]),
+             pltpu.make_async_copy(pos_hbm, pos_ref, small_sem.at[2]),
+             pltpu.make_async_copy(qg_hbm, gain_ref.at[0], small_sem.at[3]), pltpu.make_async_copy(kg_hbm, gain_ref.at[1], small_sem.at[4]))
     for cp in small:
         cp.start()
     local = o_ref.shape[0]
@@ -527,8 +529,8 @@
 
     for cp in small:
         cp.wait()
-    cos_tab, sin_tab = tabs_ref[pl.ds(0, local), :], tabs_ref[pl.ds(local, local), :]
-    gains = [tabs_ref[pl.ds(2 * local + 2 * layer + i, 1), :] for i in (0, 1)]
+    cos_tab, sin_tab = tabs_ref[0], tabs_ref[1]
+    gains = [gain_ref[i, pl.ds(layer, 1), :].astype(F32) for i in (0, 1)]
 
     def norm_rope(vals, gain):
         normed = vals * lax.rsqrt(jnp.mean(vals * vals, axis=-1, keepdims=True) + NORM_EPS) * gain
@@ -597,20 +599,20 @@
         run(blk, False, True, True)
 
 
-def attn_call(layer, pos, qkv, tabs, k_cache, v_cache, pref, prev):
+def attn_call(layer, pos, qkv, cos_tab, sin_tab, q_gain, k_gain, k_cache, v_cache, pref, prev):
     layers, local, n_rows, _ = k_cache.shape
     n_kv = 4
     n_q = 16
     vmem = pl.BlockSpec(memory_space=pltpu.VMEM)
     hbm = pl.BlockSpec(memory_space=pltpu.HBM)
-    args = [in_hbm(pos), qkv if layer == 0 else in_hbm(qkv), in_hbm(tabs), in_hbm(k_cache), in_hbm(v_cache), pltpu.with_memory_space_constraint(pref, pltpu.VMEM)]
-    in_specs = [hbm, hbm, hbm, hbm, hbm, vmem]
-    aliases = {5: 3}
+    args = [in_hbm(pos), qkv if layer == 0 else in_hbm(qkv), in_hbm(cos_tab), in_hbm(sin_tab), in_hbm(q_gain), in_hbm(k_gain), in_hbm(k_cache), in_hbm(v_cache), pltpu.with_memory_space_constraint(pref, pltpu.VMEM)]
+    in_specs = [hbm] * 8 + [vmem]
+    aliases = {8: 3}
     n_pref, n_blocks = pref.shape[0], local // SB
     if prev is not None:
         args += list(prev)
         in_specs += [hbm] * 2
-        aliases.update({6: 0, 7: 1})
+        aliases.update({9: 0, 10: 1})
     return pl.pallas_call(
         functools.partial(attn_kernel, layer, n_pref),
         out_shape=[jax.ShapeDtypeStruct(k_cache.shape, BF16)] * 2 + [jax.ShapeDtypeStruct((local, n_q * HEAD_DIM), BF16), jax.ShapeDtypeStruct(pref.shape, BF16)],
@@ -619,8 +621,8 @@
         scratch_shapes=[pltpu.VMEM((min(NBUF, max(n_blocks - n_pref, 1)) if n_pref < n_blocks else 1, 2, SB if n_pref < n_blocks else 1, n_rows, HEAD_DIM), BF16),
                         pltpu.VMEM((n_q * local, HEAD_DIM), F32), pltpu.VMEM((2, n_kv * local, HEAD_DIM), F32), pltpu.VMEM((n_q * local, HEAD_DIM), F32),
                         pltpu.VMEM((SB, n_q, n_rows), F32), pltpu.VMEM((SB, n_q, n_rows), BF16),
-                        pltpu.VMEM(qkv.shape, BF16), pltpu.VMEM(tabs.shape, F32), pltpu.SMEM(pos.shape, jnp.int32),
-                        pltpu.SemaphoreType.DMA((n_blocks, 2)), pltpu.SemaphoreType.DMA((n_blocks, 2)), pltpu.SemaphoreType.DMA((3,))],
+                        pltpu.VMEM(qkv.shape, BF16), pltpu.VMEM((2,) + cos_tab.shape, F32), pltpu.SMEM(pos.shape, jnp.int32), pltpu.VMEM((2,) + q_gain.shape, BF16),
+                        pltpu.SemaphoreType.DMA((n_blocks, 2)), pltpu.SemaphoreType.DMA((n_blocks, 2)), pltpu.SemaphoreType.DMA((6,))],
         input_output_aliases=aliases, name=f'attn_{layer}',
         compiler_params=pltpu.CompilerParams(vmem_limit_bytes=(20 if layer == 0 else 22) * 1024 * 1024),
     )(*args)
@@ -639,15 +641,14 @@
         layers, local, cache_len, n_kv, _ = k_cache.shape
         my_pos = lax.dynamic_slice_in_dim(positions, lax.axis_index('x') * local, local)
         half = HEAD_DIM // 2
-        inv_freq = jnp.power(ROPE_BASE, -2.0 * jnp.arange(half, dtype=F32) / HEAD_DIM)
-        angles = my_pos.astype(F32)[:, None] * inv_freq[None, :]
-        cos_half, sin_half = jnp.cos(angles), jnp.sin(angles)
-        gains = jnp.stack([q_gain[0], k_gain[0], q_gain[1], k_gain[1]]).astype(F32)
-        tabs = jnp.concatenate([jnp.concatenate([cos_half, cos_half], axis=1), jnp.concatenate([-sin_half, sin_half], axis=1), gains, jnp.zeros((4, HEAD_DIM), F32)])
-        tabs, my_pos, hidden = lax.optimization_barrier((tabs, my_pos, hidden))
+        inv_freq = np.power(ROPE_BASE, -2.0 * np.arange(half) / HEAD_DIM).astype(np.float32)
+        angles = my_pos.astype(F32)[:, None] * jnp.asarray(np.concatenate([inv_freq, inv_freq]))[None, :]
+        sign = jnp.asarray(np.repeat(np.array([-1.0, 1.0], np.float32), half))
+        cos_tab, sin_tab = jnp.cos(angles), jnp.sin(angles) * sign[None, :]
+        cos_tab, sin_tab, my_pos, hidden = lax.optimization_barrier((cos_tab, sin_tab, my_pos, hidden))
         k_rows = k_cache.reshape(layers, local, cache_len * n_kv, HEAD_DIM)
         v_rows = v_cache.reshape(layers, local, cache_len * n_kv, HEAD_DIM)
-        attn_tabs = (tabs, k_rows, v_rows)
+        attn_tabs = (cos_tab, sin_tab, q_gain, k_gain, k_rows, v_rows)
         caches = {'k_rows': k_rows, 'v_rows': v_rows}
         qkv, pref = chain_call(False, True, 0, 0, 8, 16, model_dim, hidden, g_attn=g_attn, wq=w_q, wk=w_k, wv=w_v, **caches)
         k_new, v_new, attn, _ = attn_call(0, my_pos, qkv, *attn_tabs, pref, None)

time: 208 us -> 206 us (level)
  no operation moved by 1% of the time
where the time goes in v6:
time: 206 us
  Pallas kernels  201 us (98%)
  other arithmetic  2.83 us (1%)
    pallas_call x3, Pallas kernels, chain_call(): pl.pallas_call(functools.partial(chain_kernel, head, tail, layer, n_pref,...  173 us
    pallas_call x2, Pallas kernels, attn_call(): pl.pallas_call(functools.partial(attn_kernel, layer, n_pref), out_shape=[...  28.2 us

profile of v6, /device:TPU:0, one launch (start us, length us, event | category | flops | bytes accessed | tf_op | source)
XLA Modules:
  0.0 206.0 jit_solution(17960520846551620325)
XLA Ops:
  0.6 1.3 fusion.1
  2.0 1.5 fusion
  3.5 18.9 %chain_01.1 = (bf16[6,64,512]{2,1,0:T(8,128)(2,1)S(1)}, bf16[8,2,8,1024,128]{4,3,2,1,0:T(8,128)(2,1)S(1)}) custom-call(bf16[256,640]{1,0:T(8,128)(2,1)} %refs_0_.1, bf16[2,640]{1,0:T(2,128)(2,1)} %refs_7_.1, bf16[2,640,2048]{2,1,0:T(8,128)(2,1)} %refs_8_.1, bf16[2,640,512]{2,1,0:T(8,128)(2,1)} %refs_9_.1, bf16[2,640,512]{2,1,0:T(8,128)(2,1)} %refs_10_.1, ...), custom_call_target="tpu_custom_call" | custom-call | tf_op jit(solution)/shard_map/chain_01/pallas_call | solution.py:488
  22.3 12.6 %attn_0.1 = (bf16[2,64,1024,128]{3,2,1,0:T(8,128)(2,1)}, bf16[2,64,1024,128]{3,2,1,0:T(8,128)(2,1)}, bf16[64,2048]{1,0:T(8,128)(2,1)S(1)}, bf16[8,2,8,1024,128]{4,3,2,1,0:T(8,128)(2,1)S(1)}) custom-call(s32[64]{0:T(128)} %get-tuple-element.19.pos_hbm, bf16[6,64,512]{2,1,0:T(8,128)(2,1)S(1)} %get-tuple-element.20.qkv_hbm, ...), custom_call_target="tpu_custom_call", output_to_operand_aliasing={{3}: (8, {})} | custom-call | tf_op jit(solution)/shard_map/attn_0/pallas_call | solution.py:616
  35.0 0.0 copy-start
  35.0 0.7 copy-done
  35.7 83.1 %chain_11.1 = (bf16[256,640]{1,0:T(8,128)(2,1)}, bf16[6,64,512]{2,1,0:T(8,128)(2,1)}, bf16[5,2,8,1024,128]{4,3,2,1,0:T(8,128)(2,1)S(1)}) custom-call(bf16[256,640]{1,0:T(8,128)(2,1)} %refs_0_.1, bf16[64,2048]{1,0:T(8,128)(2,1)} %copy-done, bf16[2,640]{1,0:T(2,128)(2,1)} %refs_2_.5, bf16[2,2048,640]{2,1,0:T(8,128)(2,1)} %refs_3_.5, ...), custom_call_target="tpu_custom_call" | custom-call | tf_op jit(solution)/shard_map/chain_11/pallas_call | solution.py:488
  118.8 15.5 %attn_1.1 = (bf16[2,64,1024,128]{3,2,1,0:T(8,128)(2,1)}, bf16[2,64,1024,128]{3,2,1,0:T(8,128)(2,1)}, bf16[64,2048]{1,0:T(8,128)(2,1)S(1)}, bf16[5,2,8,1024,128]{4,3,2,1,0:T(8,128)(2,1)S(1)}) custom-call(s32[64]{0:T(128)} %get-tuple-element.19.pos_hbm, ...), custom_call_target="tpu_custom_call", output_to_operand_aliasing={{3}: (8, {}), {0}: (9, {}), {1}: (10, {})} | custom-call | tf_op jit(solution)/shard_map/attn_1/pallas_call | solution.py:616
  134.4 70.9 %chain_10.1 = bf16[256,640]{1,0:T(8,128)(2,1)S(1)} custom-call(bf16[256,640]{1,0:T(8,128)(2,1)} %get-tuple-element.25.refs_0_, bf16[64,2048]{1,0:T(8,128)(2,1)S(1)} %get-tuple-element.30.refs_1_, bf16[2,640]{1,0:T(2,128)(2,1)} %refs_2_.5, bf16[2,2048,640]{2,1,0:T(8,128)(2,1)} %refs_3_.5, bf16[2,640,4864]{2,1,0:T(8,128)(2,1)} %refs_4_.5, ...), custom_call_target="tpu_custom_call" | custom-call | tf_op jit(solution)/shard_map/chain_10/pallas_call | solution.py:488
  205.2 0.7 copy.29
Async XLA Ops:
  35.0 0.7 copy-start

commit v7 on v6

--- a/solution.py
+++ b/solution.py
@@ -454,7 +454,7 @@
     out_shape, out_specs = [], []
     n_items = 0
     if head:
-        args += [attn, in_hbm(g_mlp), in_hbm(wo), in_hbm(wg), in_hbm(wu), in_hbm(wd)]
+        args += [in_hbm(attn), in_hbm(g_mlp), in_hbm(wo), in_hbm(wg), in_hbm(wu), in_hbm(wd)]
         in_specs += [hbm] * 6
         out_shape.append(jax.ShapeDtypeStruct(hidden.shape, hidden.dtype))
         out_specs.append(hbm)
@@ -494,7 +494,7 @@
 
 
 def attn_kernel(layer, n_pref, pos_hbm, qkv_hbm, cos_hbm, sin_hbm, qg_hbm, kg_hbm, k_hbm, v_hbm, *refs):
-    k_out, v_out, o_ref, pref, kv_slots, q_buf, kv_buf, o_buf, s_buf, p_buf, qkv_ref, tabs_ref, pos_ref, gain_ref, in_sem, out_sem, small_sem = refs[-17:]
+    k_out, v_out, o_ref, pref, kv_slots, q_buf, kv_buf, o_buf, s_buf, p_buf, qkv_ref, tabs_ref, pos_ref, gain_ref, o_vmem, in_sem, out_sem, small_sem = refs[-18:]
     small = (pltpu.make_async_copy(qkv_hbm, qkv_ref, small_sem.at[0]), pltpu.make_async_copy(cos_hbm, tabs_ref.at[0], small_sem.at[1]), pltpu.make_async_copy(sin_hbm, tabs_ref.at[1], small_sem.at[5]),
              pltpu.make_async_copy(pos_hbm, pos_ref, small_sem.at[2]),
              pltpu.make_async_copy(qg_hbm, gain_ref.at[0], small_sem.at[3]), pltpu.make_async_copy(kg_hbm, gain_ref.at[1], small_sem.at[4]))
@@ -592,7 +592,10 @@
         block_step(blk, blk < n_pref, nxt, False)
 
     for h in range(n_q):
-        o_ref[:, pl.ds(h * HEAD_DIM, HEAD_DIM)] = o_buf[pl.ds(h * local, local), :].astype(BF16)
+        o_vmem[:, pl.ds(h * HEAD_DIM, HEAD_DIM)] = o_buf[pl.ds(h * local, local), :].astype(BF16)
+    o_copy = pltpu.make_async_copy(o_vmem, o_ref, small_sem.at[6])
+    o_copy.start()
+    o_copy.wait()
     for blk in range(n_pref):
         run(blk, True, True, True)
     for blk in range(max(n_blocks - NBUF, n_pref), n_blocks):
@@ -615,14 +618,14 @@
         aliases.update({9: 0, 10: 1})
     return pl.pallas_call(
         functools.partial(attn_kernel, layer, n_pref),
-        out_shape=[jax.ShapeDtypeStruct(k_cache.shape, BF16)] * 2 + [jax.ShapeDtypeStruct((local, n_q * HEAD_DIM), BF16), jax.ShapeDtypeStruct(pref.shape, BF16)],
+        out_shape=[jax.ShapeDtypeStruct(k_cache.shape, BF16)] * 2 + [pltpu.HBM((local, n_q * HEAD_DIM), BF16), jax.ShapeDtypeStruct(pref.shape, BF16)],
         in_specs=in_specs,
-        out_specs=[hbm, hbm, vmem, vmem],
+        out_specs=[hbm, hbm, hbm, vmem],
         scratch_shapes=[pltpu.VMEM((min(NBUF, max(n_blocks - n_pref, 1)) if n_pref < n_blocks else 1, 2, SB if n_pref < n_blocks else 1, n_rows, HEAD_DIM), BF16),
                         pltpu.VMEM((n_q * local, HEAD_DIM), F32), pltpu.VMEM((2, n_kv * local, HEAD_DIM), F32), pltpu.VMEM((n_q * local, HEAD_DIM), F32),
                         pltpu.VMEM((SB, n_q, n_rows), F32), pltpu.VMEM((SB, n_q, n_rows), BF16),
-                        pltpu.VMEM(qkv.shape, BF16), pltpu.VMEM((2,) + cos_tab.shape, F32), pltpu.SMEM(pos.shape, jnp.int32), pltpu.VMEM((2,) + q_gain.shape, BF16),
-                        pltpu.SemaphoreType.DMA((n_blocks, 2)), pltpu.SemaphoreType.DMA((n_blocks, 2)), pltpu.SemaphoreType.DMA((6,))],
+                        pltpu.VMEM(qkv.shape, BF16), pltpu.VMEM((2,) + cos_tab.shape, F32), pltpu.SMEM(pos.shape, jnp.int32), pltpu.VMEM((2,) + q_gain.shape, BF16), pltpu.VMEM((local, n_q * HEAD_DIM), BF16),
+                        pltpu.SemaphoreType.DMA((n_blocks, 2)), pltpu.SemaphoreType.DMA((n_blocks, 2)), pltpu.SemaphoreType.DMA((7,))],
         input_output_aliases=aliases, name=f'attn_{layer}',
         compiler_params=pltpu.CompilerParams(vmem_limit_bytes=(20 if layer == 0 else 22) * 1024 * 1024),
     )(*args)

time: 206 us -> 206 us (level)
  no operation moved by 1% of the time
where the time goes in v7:
time: 206 us; the launch traced here: 205 us
  Pallas kernels  201 us (98%)
  other arithmetic  2.75 us (1%)
    pallas_call x3, Pallas kernels, chain_call(): pl.pallas_call(functools.partial(chain_kernel, head, tail, layer, n_pref,...  173 us
    pallas_call x2, Pallas kernels, attn_call(): pl.pallas_call(functools.partial(attn_kernel, layer, n_pref), out_shape=[...  28.3 us

profile of v7, /device:TPU:0, one launch (start us, length us, event | category | flops | bytes accessed | tf_op | source)
XLA Modules:
  0.0 205.3 jit_solution(16463195812766414567)
XLA Ops:
  0.6 1.3 fusion.1
  1.9 1.5 fusion
  3.4 18.9 %chain_01.1 = (bf16[6,64,512]{2,1,0:T(8,128)(2,1)S(1)}, bf16[8,2,8,1024,128]{4,3,2,1,0:T(8,128)(2,1)S(1)}) custom-call(bf16[256,640]{1,0:T(8,128)(2,1)} %refs_0_.1, bf16[2,640]{1,0:T(2,128)(2,1)} %refs_7_.1, bf16[2,640,2048]{2,1,0:T(8,128)(2,1)} %refs_8_.1, bf16[2,640,512]{2,1,0:T(8,128)(2,1)} %refs_9_.1, bf16[2,640,512]{2,1,0:T(8,128)(2,1)} %refs_10_.1, ...), custom_call_target="tpu_custom_call" | custom-call | tf_op jit(solution)/shard_map/chain_01/pallas_call | solution.py:488
  22.3 12.7 %attn_0.1 = (bf16[2,64,1024,128]{3,2,1,0:T(8,128)(2,1)}, bf16[2,64,1024,128]{3,2,1,0:T(8,128)(2,1)}, bf16[64,2048]{1,0:T(8,128)(2,1)}, bf16[8,2,8,1024,128]{4,3,2,1,0:T(8,128)(2,1)S(1)}) custom-call(s32[64]{0:T(128)} %get-tuple-element.19.pos_hbm, bf16[6,64,512]{2,1,0:T(8,128)(2,1)S(1)} %get-tuple-element.20.qkv_hbm, ...), custom_call_target="tpu_custom_call", output_to_operand_aliasing={{3}: (8, {})} | custom-call | tf_op jit(solution)/shard_map/attn_0/pallas_call | solution.py:619
  34.9 83.2 %chain_11.1 = (bf16[256,640]{1,0:T(8,128)(2,1)}, bf16[6,64,512]{2,1,0:T(8,128)(2,1)}, bf16[5,2,8,1024,128]{4,3,2,1,0:T(8,128)(2,1)S(1)}) custom-call(bf16[256,640]{1,0:T(8,128)(2,1)} %refs_0_.1, bf16[64,2048]{1,0:T(8,128)(2,1)} %get-tuple-element.24.refs_1_, bf16[2,640]{1,0:T(2,128)(2,1)} %refs_2_.5, bf16[2,2048,640]{2,1,0:T(8,128)(2,1)} %refs_3_.5, ...), custom_call_target="tpu_custom_call" | custom-call | tf_op jit(solution)/shard_map/chain_11/pallas_call | solution.py:488
  118.1 15.6 %attn_1.1 = (bf16[2,64,1024,128]{3,2,1,0:T(8,128)(2,1)}, bf16[2,64,1024,128]{3,2,1,0:T(8,128)(2,1)}, bf16[64,2048]{1,0:T(8,128)(2,1)}, bf16[5,2,8,1024,128]{4,3,2,1,0:T(8,128)(2,1)S(1)}) custom-call(s32[64]{0:T(128)} %get-tuple-element.19.pos_hbm, ...), custom_call_target="tpu_custom_call", output_to_operand_aliasing={{3}: (8, {}), {0}: (9, {}), {1}: (10, {})} | custom-call | tf_op jit(solution)/shard_map/attn_1/pallas_call | solution.py:619
  133.7 70.9 %chain_10.1 = bf16[256,640]{1,0:T(8,128)(2,1)S(1)} custom-call(bf16[256,640]{1,0:T(8,128)(2,1)} %get-tuple-element.25.refs_0_, bf16[64,2048]{1,0:T(8,128)(2,1)} %get-tuple-element.30.refs_1_, bf16[2,640]{1,0:T(2,128)(2,1)} %refs_2_.5, bf16[2,2048,640]{2,1,0:T(8,128)(2,1)} %refs_3_.5, bf16[2,640,4864]{2,1,0:T(8,128)(2,1)} %refs_4_.5, ...), custom_call_target="tpu_custom_call" | custom-call | tf_op jit(solution)/shard_map/chain_10/pallas_call | solution.py:488
  204.6 0.7 copy.29
